TPU v7x, 32 devices: a 4x4x1 block of a 4x4x8 slice. The times are simulated.
32 devices in a mesh: dp: 1 (over z), sp: 4 (over y), tp: 8 (over x, core).
Axes of the slice: x: 4, y: 4, z: 1, core: 2. Of those that a mesh axis runs over, the one named last changes fastest.
The devices are a block of a 4x4x8 slice.
Arguments:
- x_in: bfloat16 [8192, 8192], P(('dp', 'sp', 'tp'))
- seg_ids: int32 [8192], P(('dp', 'sp', 'tp'))
- w_zx: bfloat16 [8192, 2, 16384], P(None, None, 'tp')
- w_bc: bfloat16 [8192, 2, 1024], P(None, None, 'tp')
- w_dt: bfloat16 [8192, 256], P(None, 'tp')
- conv_x: bfloat16 [4, 16384], P(None, 'tp')
- conv_bc: bfloat16 [4, 2, 1024], P(None, None, 'tp')
- bias_x: bfloat16 [16384], P('tp')
- bias_bc: bfloat16 [2, 1024], P(None, 'tp')
- a_log: float32 [256], P('tp')
- dt_bias: float32 [256], P('tp')
- d_skip: float32 [256], P('tp')
- norm_w: bfloat16 [16384], P('tp')
- w_out: bfloat16 [16384, 8192], P('tp')
Outputs:
- output: bfloat16 [8192, 8192], P(('dp', 'sp', 'tp'))
All inputs are finite; a program needn't handle non-finite values.
Results may differ from a plain program's by a relative error of at most 0.00685.
Values are sent between devices in bfloat16 or wider.
A program may use at most 768 MiB of HBM per device.

v0:
```python
import math
import jax
import jax.numpy as jnp
from jax import lax
from jax.sharding import PartitionSpec as P

SSD_TILE = 256
CONV_WIDTH = 4
STATE_DIM = 128
NORM_EPS = 1e-5


def causal_conv(pre_rows, tail_rows, seg_rows, seg_tail, conv_w, conv_b):
    row_count = pre_rows.shape[0]
    padded = jnp.concatenate([tail_rows, pre_rows], axis=0)
    seg_pad = jnp.concatenate([seg_tail, seg_rows], axis=0)
    conv_acc = conv_b.astype(jnp.float32)
    for tap_idx in range(CONV_WIDTH):
        keep_tap = (seg_pad[tap_idx:tap_idx + row_count] == seg_rows)[:, None]
        tap_term = padded[tap_idx:tap_idx + row_count].astype(jnp.float32) * conv_w[tap_idx].astype(jnp.float32)
        conv_acc = conv_acc + jnp.where(keep_tap, tap_term, 0.0)
    return jax.nn.silu(conv_acc).astype(jnp.bfloat16)


def ssd_tile(state, tile_in, skip_gain):
    x_ssm, b_ssm, c_ssm, dt_val, log_a, seg_rows, seg_prev = tile_in
    row_count = x_ssm.shape[0]
    last_row = row_count - 1
    cum_log = jnp.cumsum(log_a, axis=0)
    causal = jnp.arange(row_count)[:, None] >= jnp.arange(row_count)[None, :]
    same_doc = ((seg_rows[:, None] == seg_rows[None, :]) & causal)[:, :, None, None]
    decay = jnp.where(same_doc, jnp.exp(jnp.where(same_doc, cum_log[:, None] - cum_log[None, :], 0.0)), 0.0)
    scores = jnp.einsum('tgn,sgn->tsg', c_ssm, b_ssm, preferred_element_type=jnp.float32)
    mix_mat = scores[..., None] * decay * dt_val[None]
    y_ssm = jnp.einsum('tsgr,sgrp->tgrp', mix_mat, x_ssm, preferred_element_type=jnp.float32)
    keep_in = (seg_rows == seg_prev)[:, None, None]
    in_fac = jnp.where(keep_in, jnp.exp(cum_log), 0.0)
    y_ssm = y_ssm + jnp.einsum('tgn,grpn->tgrp', c_ssm, state, preferred_element_type=jnp.float32) * in_fac[..., None]
    y_ssm = y_ssm + skip_gain[None, :, :, None] * x_ssm.astype(jnp.float32)
    keep_end = (seg_rows == seg_rows[last_row])[:, None, None]
    end_w = jnp.where(keep_end, jnp.exp(cum_log[last_row][None] - cum_log), 0.0) * dt_val
    carry_fac = jnp.where(seg_rows[last_row] == seg_prev, jnp.exp(cum_log[last_row]), 0.0)
    new_state = carry_fac[:, :, None, None] * state + jnp.einsum('sgrp,sgn->grpn', x_ssm * end_w[..., None], b_ssm, preferred_element_type=jnp.float32)
    return new_state, y_ssm


def block_ssd(x_ssm, b_ssm, c_ssm, dt_val, log_a, seg_rows, seg_prev, skip_gain):
    row_count, groups, per_group, head_dim = x_ssm.shape
    tile_size = math.gcd(row_count, SSD_TILE)
    n_tiles = row_count // tile_size
    seg_shift = jnp.concatenate([seg_prev[None], seg_rows[:-1]])
    tile_prev = seg_shift.reshape(n_tiles, tile_size)[:, 0]
    tiles_in = (x_ssm.reshape(n_tiles, tile_size, groups, per_group, head_dim), b_ssm.reshape(n_tiles, tile_size, groups, STATE_DIM), c_ssm.reshape(n_tiles, tile_size, groups, STATE_DIM), dt_val.reshape(n_tiles, tile_size, groups, per_group), log_a.reshape(n_tiles, tile_size, groups, per_group), seg_rows.reshape(n_tiles, tile_size), tile_prev)

    def body(state, step_in):
        return ssd_tile(state, step_in, skip_gain)

    init_state = jnp.zeros((groups, per_group, head_dim, STATE_DIM), jnp.float32)
    end_state, y_tiles = lax.scan(body, init_state, tiles_in)
    return end_state, y_tiles.reshape(row_count, groups, per_group, head_dim)


def gate_norm(y_ssm, z_gate, norm_w):
    row_count, groups, per_group, head_dim = y_ssm.shape
    group_size = per_group * head_dim
    gated = y_ssm.reshape(row_count, groups, group_size) * jax.nn.silu(z_gate.astype(jnp.float32)).reshape(row_count, groups, group_size)
    normed = gated * lax.rsqrt(jnp.mean(gated * gated, axis=-1, keepdims=True) + NORM_EPS)
    return (normed.reshape(row_count, groups * group_size) * norm_w.astype(jnp.float32)).astype(jnp.bfloat16)


def chain_state(end_state, block_decay, seq_axis, n_blocks):
    dev_index = lax.axis_index(seq_axis)
    to_next = [(src_dev, src_dev + 1) for src_dev in range(n_blocks - 1)]
    state_in = lax.ppermute(end_state, seq_axis, to_next)
    decay_in = jnp.where(dev_index == 0, 1.0, lax.ppermute(block_decay, seq_axis, to_next))
    for step_idx in range((n_blocks - 1).bit_length()):
        hop_span = 2 ** step_idx
        hop_perm = [(src_dev, src_dev + hop_span) for src_dev in range(n_blocks - hop_span)]
        prev_state = lax.ppermute(state_in, seq_axis, hop_perm)
        prev_decay = lax.ppermute(decay_in, seq_axis, hop_perm)
        has_prev = dev_index >= hop_span
        state_in = jnp.where(has_prev, decay_in[:, :, None, None] * prev_state + state_in, state_in)
        decay_in = jnp.where(has_prev, decay_in * prev_decay, decay_in)
    return state_in


def local_layer(x_blk, seg_blk, weights, seq_axis, n_blocks):
    w_zx, w_bc, w_dt, conv_x, conv_bc, bias_x, bias_bc, a_log, dt_bias, d_skip, norm_w, w_out = weights
    row_count = x_blk.shape[0]
    inner_dim = w_zx.shape[2]
    group_width = w_bc.shape[2]
    heads = w_dt.shape[1]
    groups = group_width // STATE_DIM
    per_group = heads // groups
    head_dim = inner_dim // heads
    halo_len = CONV_WIDTH - 1
    zx_proj = jnp.einsum('ld,dkc->lkc', x_blk, w_zx, preferred_element_type=jnp.float32).astype(jnp.bfloat16)
    bc_pre = jnp.einsum('ld,dkc->lkc', x_blk, w_bc, preferred_element_type=jnp.float32).astype(jnp.bfloat16).reshape(row_count, 2 * group_width)
    dt_raw = jnp.dot(x_blk, w_dt, preferred_element_type=jnp.float32).astype(jnp.bfloat16)
    x_pre = zx_proj[:, 1]
    to_next = [(src_dev, src_dev + 1) for src_dev in range(n_blocks - 1)]
    tail_x = lax.ppermute(x_pre[row_count - halo_len:], seq_axis, to_next)
    tail_bc = lax.ppermute(bc_pre[row_count - halo_len:], seq_axis, to_next)
    tail_seg = lax.ppermute(seg_blk[row_count - halo_len:], seq_axis, to_next)
    x_act = causal_conv(x_pre, tail_x, seg_blk, tail_seg, conv_x, bias_x)
    bc_act = causal_conv(bc_pre, tail_bc, seg_blk, tail_seg, conv_bc.reshape(CONV_WIDTH, 2 * group_width), bias_bc.reshape(2 * group_width))
    x_ssm = x_act.reshape(row_count, groups, per_group, head_dim)
    b_ssm = bc_act[:, :group_width].reshape(row_count, groups, STATE_DIM)
    c_ssm = bc_act[:, group_width:].reshape(row_count, groups, STATE_DIM)
    dt_val = jax.nn.softplus(dt_raw.astype(jnp.float32) + dt_bias).reshape(row_count, groups, per_group)
    log_a = -jnp.exp(a_log).reshape(groups, per_group) * dt_val
    seg_prev = tail_seg[halo_len - 1]
    end_state, y_local = block_ssd(x_ssm, b_ssm, c_ssm, dt_val, log_a, seg_blk, seg_prev, d_skip.reshape(groups, per_group))
    cum_blk = jnp.cumsum(log_a, axis=0)
    block_decay = jnp.where(seg_blk[row_count - 1] == seg_prev, jnp.exp(cum_blk[row_count - 1]), 0.0)
    state_in = chain_state(end_state, block_decay, seq_axis, n_blocks)
    keep_blk = (seg_blk == seg_prev)[:, None, None]
    corr_fac = jnp.where(keep_blk, jnp.exp(cum_blk), 0.0)
    y_ssm = y_local + jnp.einsum('tgn,grpn->tgrp', c_ssm, state_in, preferred_element_type=jnp.float32) * corr_fac[..., None]
    y_norm = gate_norm(y_ssm, zx_proj[:, 0], norm_w)
    return jnp.dot(y_norm, w_out, preferred_element_type=jnp.float32)


def solution(mesh):
    seq_blocks = mesh.shape['sp']
    token_spec = P(('dp', 'sp', 'tp'), None)
    seg_spec = P(('dp', 'sp', 'tp'))
    weight_specs = (P(None, None, 'tp'), P(None, None, 'tp'), P(None, 'tp'), P(None, 'tp'), P(None, None, 'tp'), P('tp'), P(None, 'tp'), P('tp'), P('tp'), P('tp'), P('tp'), P('tp', None))

    def body(x_loc, seg_loc, w_zx, w_bc, w_dt, conv_x, conv_bc, bias_x, bias_bc, a_log, dt_bias, d_skip, norm_w, w_out):
        x_blk = lax.all_gather(x_loc, 'tp', axis=0, tiled=True)
        seg_blk = lax.all_gather(seg_loc, 'tp', axis=0, tiled=True)
        weights = (w_zx, w_bc, w_dt, conv_x, conv_bc, bias_x, bias_bc, a_log, dt_bias, d_skip, norm_w, w_out)
        out_part = local_layer(x_blk, seg_blk, weights, 'sp', seq_blocks)
        out_loc = lax.psum_scatter(out_part, 'tp', scatter_dimension=0, tiled=True)
        return (x_loc.astype(jnp.float32) + out_loc).astype(jnp.bfloat16)

    return jax.shard_map(body, mesh=mesh, in_specs=(token_spec, seg_spec) + weight_specs, out_specs=token_spec, check_vma=False)
```

profile of v0, /device:TPU:97, one launch (start us, length us, event | category | flops | bytes accessed | tf_op | source)
XLA Modules:
  0.0 1554.1 jit_solution(7842834657642764762)
XLA Ops:
  7.4 18.9 %all-gather = s32[8,1,256]{2,1,0:T(1,128)S(1)} all-gather(s32[1,1,256]{2,1,0:T(1,128)} %bitcast.281), channel_id=1, replica_groups=mesh['dp'=1,'sp'=4,'tp'=8] {'tp'}, dimensions={0}, use_global_device_ids=true | all-gather | bytes 9216 | tf_op jit(solution)/shard_map/all_gather | solution.py:132
  26.3 3.8 collective-permute-start
  40.6 126.9 %all-gather.3.cloned.1.call-done = bf16[2048,8192]{1,0:T(8,128)(2,1)} async-done(((bf16[256,8192]{1,0:T(8,128)(2,1)}), bf16[2048,8192]{1,0:T(8,128)(2,1)}) %all-gather.3.cloned.1.call-update) | async-done | bytes 33554448 | tf_op jit(solution)/shard_map/all_gather | solution.py:131
  167.5 16.3 %fusion.76 = bf16[2048,2,128]{2,0,1:T(8,128)(2,1)S(1)} fusion(bf16[8192,2,128]{2,1,0:T(2,128)(2,1)} %param.19, bf16[2048,8192]{1,0:T(8,128)(2,1)} %all-gather.3.cloned.1.call-done), kind=kOutput, calls=%fused_computation.96 | convolution fusion | flops 8590458880 | bytes 38797312 | tf_op jit(solution)/shard_map/ld,dkc->lkc/dot_general | solution.py:98
  185.4 4.2 collective-permute-start.2
  189.6 154.0 %fusion.64 = bf16[2048,2,2048]{2,0,1:T(8,128)(2,1)} fusion(bf16[8192,2,2048]{2,1,0:T(2,128)(2,1)} %param.18, bf16[2048,8192]{1,0:T(8,128)(2,1)} %all-gather.3.cloned.1.call-done), kind=kOutput, calls=%fused_computation.86 | convolution fusion | flops 137447342080 | bytes 117440512 | tf_op jit(solution)/shard_map/ld,dkc->lkc/dot_general | solution.py:97
  343.6 8.3 slice_bitcast_fusion.1
  352.0 16.2 %broadcast_multiply_fusion = (f32[2048,32]{0,1:T(8,128)S(1)}, f32[2048,32]{0,1:T(8,128)S(1)}) fusion(f32[32]{0:T(128)S(1)} %copy-done.17, f32[32]{0:T(128)S(1)} %copy-done.16, bf16[2048,8192]{1,0:T(8,128)(2,1)} %all-gather.3.cloned.1.call-done, bf16[8192,32]{0,1:T(8,128)(2,1)S(1)} %copy-done), kind=kOutput, calls=%fused_computation.116 | convolution fusion | flops 1074397184 | bytes 34603264 | tf_op jit(solution)/shard_map/dot_general | solution.py:99
  371.6 2.6 collective-permute-start.1
  374.3 3.5 multiply_convert_fusion.1
  380.0 26.1 %multiply_convert_fusion = bf16[2048,2048]{1,0:T(8,128)(2,1)} fusion(bf16[2048,2048]{1,0:T(8,128)(2,1)} %slice_bitcast_fusion.1, bf16[3,2048]{1,0:T(4,128)(2,1)S(1)} %collective-permute-done.1, f32[2048]{0:T(1024)S(1)} %bitcast.277, f32[2048]{0:T(1024)S(1)} %bitcast.278, f32[2048]{0:T(1024)S(1)} %bitcast.276, f32[2048]{0:T(1024)S(1)} %bitcast.275, ...), kind=kLoop, calls=%fused_computation.83 | loop fusion | flops 121634816 | bytes 16836608 | tf_op jit(solution)/shard_map/convert_element_type | solution.py:22
  406.1 24.4 %reshape.410 = bf16[8,256,1,32,64]{4,3,1,0,2:T(8,128)(2,1)} reshape(bf16[2048,2048]{1,0:T(8,128)(2,1)} %multiply_convert_fusion) | data formatting | bytes 16777216 | tf_op jit(solution)/shard_map/reshape;reshape | solution.py:53
  430.5 19.6 %copy.90 = bf16[8,256,1,32,64]{1,4,3,2,0:T(8,128)(2,1)} copy(bf16[8,256,1,32,64]{4,3,1,0,2:T(8,128)(2,1)} %reshape.410) | data formatting | bytes 16777216
  450.1 536.6 %while.13 = (s32[]{:T(128)}, f32[1,32,64,128]{3,2,1,0:T(8,128)S(1)}, f32[8,256,1,32,64]{1,0,4,3,2:T(8,128)}, s32[8,256]{1,0:T(8,128)}, s32[8]{0:T(128)S(1)}, /*i...) while((s32[]{:T(128)}, ...), condition=%wide.region_3.4_spmd.clone, body=%wide.region_0.3_spmd.clone.sunk | while | flops 570131072 | bytes 23409008 | solution.py:59
  461.4 4.6 fusion.133
  470.0 47.3 %dynamic_update_slice.6 = f32[8,256,1,32,64]{1,0,4,3,2:T(8,128)} dynamic-update-slice(f32[8,256,1,32,64]{1,0,4,3,2:T(8,128)} %get-tuple-element.293, f32[1,256,1,32,64]{1,0,4,3,2:T(1,128)S(1)} %copy.150, s32[]{:T(128)S(6)} %copy.155, s32[]{:T(128)} %constant.30.clone.1..sunk, s32[]{:T(128)} %constant.30.clone.1..sunk, s32[]{:T(128)} %constant.30.clone.1..sunk, s32[]{:T(128)} %constant.30.clone.1..sunk) | dynamic-update-slice | bytes 4194308 | tf_op jit(solution)/shard_map/while/body/jit(dynamic_update_index_in_dim)/dynamic_update_slice | solution.py:59
  528.6 4.6 fusion.133
  533.1 2.2 copy.150
  537.1 47.3 %dynamic_update_slice.6 = f32[8,256,1,32,64]{1,0,4,3,2:T(8,128)} dynamic-update-slice(f32[8,256,1,32,64]{1,0,4,3,2:T(8,128)} %get-tuple-element.293, f32[1,256,1,32,64]{1,0,4,3,2:T(1,128)S(1)} %copy.150, s32[]{:T(128)S(6)} %copy.155, s32[]{:T(128)} %constant.30.clone.1..sunk, s32[]{:T(128)} %constant.30.clone.1..sunk, s32[]{:T(128)} %constant.30.clone.1..sunk, s32[]{:T(128)} %constant.30.clone.1..sunk) | dynamic-update-slice | bytes 4194308 | tf_op jit(solution)/shard_map/while/body/jit(dynamic_update_index_in_dim)/dynamic_update_slice | solution.py:59
  595.7 4.6 fusion.133
  604.2 47.3 %dynamic_update_slice.6 = f32[8,256,1,32,64]{1,0,4,3,2:T(8,128)} dynamic-update-slice(f32[8,256,1,32,64]{1,0,4,3,2:T(8,128)} %get-tuple-element.293, f32[1,256,1,32,64]{1,0,4,3,2:T(1,128)S(1)} %copy.150, s32[]{:T(128)S(6)} %copy.155, s32[]{:T(128)} %constant.30.clone.1..sunk, s32[]{:T(128)} %constant.30.clone.1..sunk, s32[]{:T(128)} %constant.30.clone.1..sunk, s32[]{:T(128)} %constant.30.clone.1..sunk) | dynamic-update-slice | bytes 4194308 | tf_op jit(solution)/shard_map/while/body/jit(dynamic_update_index_in_dim)/dynamic_update_slice | solution.py:59
  662.8 4.4 fusion.133
  671.2 47.3 %dynamic_update_slice.6 = f32[8,256,1,32,64]{1,0,4,3,2:T(8,128)} dynamic-update-slice(f32[8,256,1,32,64]{1,0,4,3,2:T(8,128)} %get-tuple-element.293, f32[1,256,1,32,64]{1,0,4,3,2:T(1,128)S(1)} %copy.150, s32[]{:T(128)S(6)} %copy.155, s32[]{:T(128)} %constant.30.clone.1..sunk, s32[]{:T(128)} %constant.30.clone.1..sunk, s32[]{:T(128)} %constant.30.clone.1..sunk, s32[]{:T(128)} %constant.30.clone.1..sunk) | dynamic-update-slice | bytes 4194308 | tf_op jit(solution)/shard_map/while/body/jit(dynamic_update_index_in_dim)/dynamic_update_slice | solution.py:59
  729.8 4.5 fusion.133
  734.3 2.2 copy.150
  738.2 47.3 %dynamic_update_slice.6 = f32[8,256,1,32,64]{1,0,4,3,2:T(8,128)} dynamic-update-slice(f32[8,256,1,32,64]{1,0,4,3,2:T(8,128)} %get-tuple-element.293, f32[1,256,1,32,64]{1,0,4,3,2:T(1,128)S(1)} %copy.150, s32[]{:T(128)S(6)} %copy.155, s32[]{:T(128)} %constant.30.clone.1..sunk, s32[]{:T(128)} %constant.30.clone.1..sunk, s32[]{:T(128)} %constant.30.clone.1..sunk, s32[]{:T(128)} %constant.30.clone.1..sunk) | dynamic-update-slice | bytes 4194308 | tf_op jit(solution)/shard_map/while/body/jit(dynamic_update_index_in_dim)/dynamic_update_slice | solution.py:59
  796.8 4.5 fusion.133
  805.3 47.3 %dynamic_update_slice.6 = f32[8,256,1,32,64]{1,0,4,3,2:T(8,128)} dynamic-update-slice(f32[8,256,1,32,64]{1,0,4,3,2:T(8,128)} %get-tuple-element.293, f32[1,256,1,32,64]{1,0,4,3,2:T(1,128)S(1)} %copy.150, s32[]{:T(128)S(6)} %copy.155, s32[]{:T(128)} %constant.30.clone.1..sunk, s32[]{:T(128)} %constant.30.clone.1..sunk, s32[]{:T(128)} %constant.30.clone.1..sunk, s32[]{:T(128)} %constant.30.clone.1..sunk) | dynamic-update-slice | bytes 4194308 | tf_op jit(solution)/shard_map/while/body/jit(dynamic_update_index_in_dim)/dynamic_update_slice | solution.py:59
  863.9 4.6 fusion.133
  872.4 47.3 %dynamic_update_slice.6 = f32[8,256,1,32,64]{1,0,4,3,2:T(8,128)} dynamic-update-slice(f32[8,256,1,32,64]{1,0,4,3,2:T(8,128)} %get-tuple-element.293, f32[1,256,1,32,64]{1,0,4,3,2:T(1,128)S(1)} %copy.150, s32[]{:T(128)S(6)} %copy.155, s32[]{:T(128)} %constant.30.clone.1..sunk, s32[]{:T(128)} %constant.30.clone.1..sunk, s32[]{:T(128)} %constant.30.clone.1..sunk, s32[]{:T(128)} %constant.30.clone.1..sunk) | dynamic-update-slice | bytes 4194308 | tf_op jit(solution)/shard_map/while/body/jit(dynamic_update_index_in_dim)/dynamic_update_slice | solution.py:59
  931.0 4.5 fusion.133
  939.4 47.3 %dynamic_update_slice.6 = f32[8,256,1,32,64]{1,0,4,3,2:T(8,128)} dynamic-update-slice(f32[8,256,1,32,64]{1,0,4,3,2:T(8,128)} %get-tuple-element.293, f32[1,256,1,32,64]{1,0,4,3,2:T(1,128)S(1)} %copy.150, s32[]{:T(128)S(6)} %copy.155, s32[]{:T(128)} %constant.30.clone.1..sunk, s32[]{:T(128)} %constant.30.clone.1..sunk, s32[]{:T(128)} %constant.30.clone.1..sunk, s32[]{:T(128)} %constant.30.clone.1..sunk) | dynamic-update-slice | bytes 4194308 | tf_op jit(solution)/shard_map/while/body/jit(dynamic_update_index_in_dim)/dynamic_update_slice | solution.py:59
  986.8 4.0 collective-permute-start.5
  993.4 9.1 reduce-window.16
  1003.4 8.0 collective-permute-done.5
  1011.4 4.3 collective-permute-start.6
  1015.9 7.8 broadcast_select_fusion.3
  1023.7 2.2 collective-permute-start.3
  1025.9 10.7 collective-permute-done.3
  1038.0 5.1 collective-permute-start.7
  1045.4 18.0 %collective-permute-done.4 = f32[1,32]{1,0:T(1,128)S(1)} collective-permute-done((f32[1,32]{1,0:T(1,128)S(1)}, f32[1,32]{1,0:T(1,128)S(1)}, u32[]{:S(2)}, u32[]{:S(2)}) %collective-permute-start.4) | collective-permute-done | bytes 160 | tf_op jit(solution)/shard_map/ppermute | solution.py:80
  1063.4 18.1 %reshape.374 = f32[2048,1,32,64]{0,3,2,1:T(8,128)} reshape(f32[8,256,1,32,64]{1,0,4,3,2:T(8,128)} %get-tuple-element.63) | data formatting | bytes 33554432 | tf_op jit(solution)/shard_map/reshape | solution.py:60
  1081.5 10.5 fusion.62
  1092.0 17.6 %copy.101 = f32[2048,1,2048]{2,0,1:T(8,128)} copy(f32[2048,1,2048]{0,2,1:T(8,128)} %bitcast.254) | data formatting | bytes 33554432 | tf_op jit(solution)/shard_map/reshape | solution.py:66
  1109.5 10.4 multiply_reduce_fusion
  1120.0 91.3 %fusion.71 = f32[2048,8192]{1,0:T(8,128)} fusion(bf16[2048,8192]{1,0:T(8,128)(2,1)} %param.29, f32[2048]{0:T(1024)S(1)} %convert_element_type.167, f32[2048]{0:T(1024)S(1)} %add_rsqrt_fusion, f32[2048,1,2048]{2,0,1:T(8,128)} %copy.101, bf16[2048,2,2048]{2,0,1:T(8,128)(2,1)} %fusion.64), kind=kOutput, calls=%fused_computation.89 | convolution fusion | flops 68757225472 | bytes 125845504 | tf_op jit(solution)/shard_map/dot_general | solution.py:121
  1211.4 328.0 %reduce-scatter.2.cloned.1.call-done = f32[256,8192]{1,0:T(8,128)} async-done(((f32[2048,8192]{1,0:T(8,128)}), f32[256,8192]{1,0:T(8,128)}) %reduce-scatter.2.cloned.1.call-update) | async-done | bytes 8388624 | tf_op jit(solution)/shard_map/reduce_scatter | solution.py:135
  1539.4 7.7 add_convert_fusion
  (309 shorter events, 131.4 us)
Async XLA Ops:
  6.5 345.3 %copy-start = (bf16[8192,32]{0,1:T(8,128)(2,1)S(1)}, bf16[8192,32]{0,1:T(8,128)(2,1)}, u32[]{:S(2)}) copy-start(bf16[8192,32]{0,1:T(8,128)(2,1)} %param.20) | copy-start | bytes 1572868
  6.6 161.0 %all-gather.3.cloned.1.call-start = ((), (), s32[]{:S(2)}) async-start(), calls=%async_computation.1 | async-start | bytes 37748736 | tf_op jit(solution)/shard_map/all_gather | solution.py:131
  7.3 1532.1 %reduce-scatter.2.cloned.1.call-start = ((), (), s32[]{:S(2)}) async-start(), calls=%async_computation.2 | async-start | bytes 75497472 | tf_op jit(solution)/shard_map/reduce_scatter | solution.py:135
  26.2 157.6 %copy-start.7 = (s32[8,1,256]{2,1,0:T(1,128)}, s32[8,1,256]{2,1,0:T(1,128)S(1)}, u32[]{:S(2)}) copy-start(s32[8,1,256]{2,1,0:T(1,128)S(1)} %all-gather) | copy-start | bytes 24580
  26.3 10.9 collective-permute-start
  183.8 1.0 copy-start.5
  185.4 188.8 %collective-permute-start.2 = (bf16[3,256]{1,0:T(4,128)(2,1)}, bf16[3,256]{1,0:T(4,128)(2,1)}, u32[]{:S(2)}, u32[]{:S(2)}) collective-permute-start(bf16[3,256]{1,0:T(4,128)(2,1)} %slice_bitcast_fusion.4), channel_id=1, source_target_pairs={{0,8},{8,16},{16,24},{1,9},{9,17},{17,25},{2,10},{10,18},{18,26},{... | collective-permute-start | bytes 4616 | tf_op jit(solution)/shard_map/ppermute | solution.py:103
  343.6 8.3 copy-start.16
  343.6 8.3 copy-start.17
  351.9 17.1 %copy-start.6 = (bf16[2048,2,128]{2,0,1:T(8,128)(2,1)S(1)}, bf16[2048,2,128]{2,0,1:T(8,128)(2,1)}, u32[]{:S(2)}) copy-start(bf16[2048,2,128]{2,0,1:T(8,128)(2,1)} %copy-done.5) | copy-start | bytes 3145732
  351.9 22.4 %copy-start.13 = (pred[2048]{0:T(1024)(128)(4,1)S(1)}, pred[2048]{0:T(1024)(128)(4,1)}, u32[]{:S(2)}) copy-start(pred[2048]{0:T(1024)(128)(4,1)} %get-tuple-element.183) | copy-start | bytes 6148
  351.9 22.4 %copy-start.14 = (pred[2048]{0:T(1024)(128)(4,1)S(1)}, pred[2048]{0:T(1024)(128)(4,1)}, u32[]{:S(2)}) copy-start(pred[2048]{0:T(1024)(128)(4,1)} %get-tuple-element.184) | copy-start | bytes 6148
  351.9 22.4 %copy-start.15 = (pred[2048]{0:T(1024)(128)(4,1)S(1)}, pred[2048]{0:T(1024)(128)(4,1)}, u32[]{:S(2)}) copy-start(pred[2048]{0:T(1024)(128)(4,1)} %get-tuple-element.185) | copy-start | bytes 6148
  351.9 22.4 %copy-start.19 = (f32[256]{0:T(256)S(1)}, f32[256]{0:T(256)}, u32[]{:S(2)}) copy-start(f32[256]{0:T(256)} %get-tuple-element.187) | copy-start | bytes 3076
  351.9 22.4 %copy-start.20 = (f32[256]{0:T(256)S(1)}, f32[256]{0:T(256)}, u32[]{:S(2)}) copy-start(f32[256]{0:T(256)} %get-tuple-element.188) | copy-start | bytes 3076
  351.9 22.4 %copy-start.21 = (f32[256]{0:T(256)S(1)}, f32[256]{0:T(256)}, u32[]{:S(2)}) copy-start(f32[256]{0:T(256)} %get-tuple-element.189) | copy-start | bytes 3076
  351.9 22.4 %copy-start.22 = (f32[256]{0:T(256)S(1)}, f32[256]{0:T(256)}, u32[]{:S(2)}) copy-start(f32[256]{0:T(256)} %get-tuple-element.190) | copy-start | bytes 3076
  351.9 22.4 %copy-start.24 = (f32[256]{0:T(256)S(1)}, f32[256]{0:T(256)}, u32[]{:S(2)}) copy-start(f32[256]{0:T(256)} %bitcast_convert_fusion.4) | copy-start | bytes 3076
  368.1 11.8 copy-start.8
  368.1 11.8 copy-start.9
  368.2 11.8 copy-start.10
  368.2 11.8 copy-start.11
  368.2 11.8 copy-start.12
  371.6 8.3 collective-permute-start.1
  377.8 1.1 copy-start.3
  430.5 19.6 %copy-start.2 = (f32[1,32,64,128]{3,2,1,0:T(8,128)S(1)}, f32[1,32,64,128]{3,2,1,0:T(8,128)}, u32[]{:S(2)}) copy-start(f32[1,32,64,128]{3,2,1,0:T(8,128)} %custom-call) | copy-start | bytes 3145732
  430.5 19.6 %copy-start.25 = (s32[8]{0:T(128)S(1)}, s32[8]{0:T(128)}, u32[]{:S(2)}) copy-start(s32[8]{0:T(128)} %slice_reduce_fusion.2) | copy-start | bytes 100
  430.5 19.6 %copy-start.26 = (f32[32]{0:T(128)S(1)}, f32[32]{0:T(128)}, u32[]{:S(2)}) copy-start(f32[32]{0:T(128)} %param.27) | copy-start | bytes 388
  450.1 565.8 %copy-start.18 = (pred[2048]{0:T(1024)(128)(4,1)S(1)}, pred[2048]{0:T(1024)(128)(4,1)}, u32[]{:S(2)}) copy-start(pred[2048]{0:T(1024)(128)(4,1)} %get-tuple-element.186) | copy-start | bytes 6148
  986.8 56.4 %copy-start.23 = (bf16[2048]{0:T(1024)(128)(2,1)S(1)}, bf16[2048]{0:T(1024)(128)(2,1)}, u32[]{:S(2)}) copy-start(bf16[2048]{0:T(1024)(128)(2,1)} %param.28) | copy-start | bytes 12292
  986.8 24.6 %collective-permute-start.5 = (f32[1,32,64,128]{3,2,1,0:T(8,128)S(1)}, f32[1,32,64,128]{3,2,1,0:T(8,128)}, u32[]{:S(2)}, u32[]{:S(2)}) collective-permute-start(f32[1,32,64,128]{3,2,1,0:T(8,128)S(1)} %get-tuple-element.64), channel_id=1, source_target_pairs={{0,8},{8,16},{16,24},{1,9},{9,17},{17,25},{2,10},{10,18},{18,26},{... | collective-permute-start | bytes 3145736 | tf_op jit(solution)/shard_map/ppermute | solution.py:74
  1011.4 25.2 %collective-permute-start.6 = (f32[1,32,64,128]{3,2,1,0:T(8,128)}, f32[1,32,64,128]{3,2,1,0:T(8,128)S(1)}, u32[]{:S(2)}, u32[]{:S(2)}) collective-permute-start(f32[1,32,64,128]{3,2,1,0:T(8,128)} %collective-permute-done.5), channel_id=1, source_target_pairs={{0,8},{8,16},{16,24},{1,9},{9,17},{17,25},{2,10},{10,18},{18,26},{... | collective-permute-start | bytes 3145736 | tf_op jit(solution)/shard_map/ppermute | solution.py:79
  1023.7 12.8 collective-permute-start.3
  1038.0 43.5 %collective-permute-start.7 = (f32[1,32,64,128]{3,2,1,0:T(8,128)S(1)}, f32[1,32,64,128]{3,2,1,0:T(8,128)S(1)}, u32[]{:S(2)}, u32[]{:S(2)}) collective-permute-start(f32[1,32,64,128]{3,2,1,0:T(8,128)S(1)} %add_select_fusion.1), channel_id=1, source_target_pairs={{0,16},{8,24},{1,17},{9,25},{2,18},{10,26},{3,19},{11,27},{4,20},{... | collective-permute-start | bytes 3145736 | tf_op jit(solution)/shard_map/ppermute | solution.py:79
  1043.2 20.3 %collective-permute-start.4 = (f32[1,32]{1,0:T(1,128)S(1)}, f32[1,32]{1,0:T(1,128)S(1)}, u32[]{:S(2)}, u32[]{:S(2)}) collective-permute-start(f32[1,32]{1,0:T(1,128)S(1)} %broadcast_select_fusion.5), channel_id=1, source_target_pairs={{0,8},{8,16},{16,24},{1,9},{9,17},{17,25},{2,10},{10,18},{18,26},{... | collective-permute-start | bytes 392 | tf_op jit(solution)/shard_map/ppermute | solution.py:80
  1063.4 18.1 %copy-start.4 = (bf16[2048,256]{1,0:T(8,128)(2,1)S(1)}, bf16[2048,256]{1,0:T(8,128)(2,1)}, u32[]{:S(2)}) copy-start(bf16[2048,256]{1,0:T(8,128)(2,1)} %copy-done.3) | copy-start | bytes 3145732
  1211.4 335.7 %copy-start.1 = (bf16[8192,32]{0,1:T(8,128)(2,1)S(1)}, bf16[8192,32]{0,1:T(8,128)(2,1)}, u32[]{:S(2)}) copy-start(bf16[8192,32]{0,1:T(8,128)(2,1)} %param.20) | copy-start | bytes 1572868
Sparse Core Ops, SparseCore 0:
  9.0 158.5 all-gather.2
  1211.5 327.8 reduce-scatter.1
where the time goes:
time: 1570 us; the launch traced here: 1550 us
  local copies, waits for them, and re-layouts  532 us (34%)
  waiting for transfers between devices  492 us (31%)
  matrix products  357 us (23%)
  other arithmetic  99.5 us (6%)
  starting transfers between devices  28.1 us (2%)
  blocking collectives  18.9 us (1%)
    dynamic_update_slice x16, local copies, waits for them, and re-layouts, block_ssd(): end_state, y_tiles = lax.scan(body, init_state, tiles_in)  396 us
    reduce_scatter x1, waiting for transfers between devices, body(): out_loc = lax.psum_scatter(out_part, 'tp', scatter_dimension=0, tiled=True)  328 us
    dot_general x1, matrix products, local_layer(): jnp.einsum('ld,dkc->lkc', x_blk, w_zx, preferred_element_type=jnp.float32)  154 us
    all_gather x1, waiting for transfers between devices, body(): x_blk = lax.all_gather(x_loc, 'tp', axis=0, tiled=True)  127 us
    dot_general x1, matrix products, local_layer(): return jnp.dot(y_norm, w_out, preferred_element_type=jnp.float32)  91.3 us
    dot_general x8, matrix products, ssd_tile(): jnp.einsum('tsgr,sgrp->tgrp', mix_mat, x_ssm, preferred_element_type=jnp....  36.2 us
  transfers between devices with their start and end apart: 10, of which 5 were waited for; matrix products, arithmetic and copies ran while one was open for 15% of the time, Pallas kernels for 0%

commit v1 on v0

v1 whole, which is shorter than its diff:
```python
import functools
import jax
import jax.numpy as jnp
from jax import lax
from jax.experimental import pallas as pl
from jax.experimental.pallas import tpu as pltpu
from jax.sharding import PartitionSpec as P

MESH = pl.DeviceIdType.MESH
NORM_EPS = 1e-5
LOG2E = 1.4426950408889634
F32 = jnp.float32
BF16 = jnp.bfloat16
HI = lax.Precision.HIGHEST
NEG = -1e30


def silu(v):
    return v * (1.0 / (1.0 + jnp.exp(-v)))


def head_lanes(cols, tile_idx, head_dim, rows):
    per = 128 // head_dim
    lane = lax.broadcasted_iota(jnp.int32, (rows, 128), 1)
    out = jnp.broadcast_to(cols[:, tile_idx * per:tile_idx * per + 1], (rows, 128))
    for j in range(1, per):
        nxt = jnp.broadcast_to(cols[:, tile_idx * per + j:tile_idx * per + j + 1], (rows, 128))
        out = jnp.where(lane >= j * head_dim, nxt, out)
    return out


def expand_heads(row, head_dim):
    heads = row.shape[1]
    width = heads * head_dim
    eye = (lax.broadcasted_iota(jnp.int32, (heads, width), 1) // head_dim == lax.broadcasted_iota(jnp.int32, (heads, width), 0)).astype(F32)
    return jnp.dot(row, eye, precision=HI, preferred_element_type=F32)


def phase_a_kernel(q, heads, inner, gw, x_ref, bc_ref, dt_ref, seg_ref, tailx_ref, tailbc_ref, tailseg_ref, cw_ref, cb_ref, alog_ref, dtb_ref,
                   xact_ref, bcact_ref, cum_ref, cl_ref, sloc_ref, send_ref, dec_ref, pad, xw, state, segtail):
    c = pl.program_id(0)
    head_dim = inner // heads
    width = inner + gw

    @pl.when(c == 0)
    def _():
        pad[0:8, 0:inner] = tailx_ref[...].astype(F32)
        pad[0:8, inner:inner + gw // 2] = tailbc_ref[0].astype(F32)
        pad[0:8, inner + gw // 2:width] = tailbc_ref[1].astype(F32)
        segtail[...] = tailseg_ref[...]
        state[...] = jnp.zeros_like(state)
        dec_ref[...] = jnp.ones_like(dec_ref)

    @pl.when(c > 0)
    def _():
        pad[0:8, :] = pad[q:q + 8, :]

    pad[8:q + 8, 0:inner] = x_ref[0].astype(F32)
    pad[8:q + 8, inner:inner + gw // 2] = bc_ref[0].astype(F32)
    pad[8:q + 8, inner + gw // 2:width] = bc_ref[1].astype(F32)
    seg_row = seg_ref[...]
    prev_row = segtail[...]
    ext = jnp.concatenate([prev_row, seg_row], axis=1)
    segtail[...] = seg_row[:, q - 128:]
    seg_last = seg_row[:, q - 1:q]
    seg_prev = prev_row[:, 127:128]
    keeps = []
    for j in range(1, 4):
        shifted = ext[:, 128 - j:128 - j + q]
        keep_row = jnp.where(shifted == seg_row, 1.0, 0.0)
        keeps.append(jnp.broadcast_to(keep_row, (128, q)).T)
    for i in range(width // 128):
        cols = slice(i * 128, (i + 1) * 128)
        acc = cb_ref[0:1, cols] + pad[8:q + 8, cols] * cw_ref[3:4, cols]
        for j in range(1, 4):
            tap = pad[8 - j:q + 8 - j, cols] * cw_ref[3 - j:4 - j, cols]
            acc = acc + tap * keeps[j - 1]
        act = silu(acc).astype(BF16)
        if i * 128 < inner:
            xact_ref[:, cols] = act
        else:
            bcact_ref[:, i * 128 - inner:(i + 1) * 128 - inner] = act
    raw = dt_ref[...].astype(F32) + dtb_ref[...]
    dt = jnp.maximum(raw, 0.0) + jnp.log1p(jnp.exp(-jnp.abs(raw)))
    log_a = dt * (alog_ref[...] * LOG2E)
    tri = (lax.broadcasted_iota(jnp.int32, (q, q), 0) <= lax.broadcasted_iota(jnp.int32, (q, q), 1)).astype(F32)
    cum = jnp.dot(log_a, tri, precision=HI, preferred_element_type=F32)
    cl = cum - jnp.log(dt) * LOG2E
    cum_ref[...] = cum
    cl_ref[...] = cl
    cum_last = cum[:, q - 1:q]
    end_w = jnp.where(seg_row == seg_last, jnp.exp2(cum_last - cum), 0.0) * dt
    carry = jnp.where(seg_last == seg_prev, jnp.exp2(cum_last), 0.0)
    end_cols = end_w.T
    carry_lane = expand_heads(jnp.broadcast_to(carry, (heads, 128)).T[0:8, :], head_dim)[0:1, :]
    for i in range(inner // 128):
        cols = slice(i * 128, (i + 1) * 128)
        xw[:, cols] = (xact_ref[:, cols].astype(F32) * head_lanes(end_cols, i, head_dim, q)).astype(BF16)
    sloc_ref[0] = state[...]
    b_t = bcact_ref[:, 0:gw // 2].T
    new_state = carry_lane * state[...] + jnp.dot(b_t, xw[...], preferred_element_type=F32)
    state[...] = new_state
    send_ref[...] = new_state
    dec_ref[...] = dec_ref[...] * carry_lane


def phase_a(zx, bc_pre, dt_t, seg_row, tail_x, tail_bc, tail_seg, conv_w, conv_b, neg_a, dt_bias, q=256):
    _, t, inner = zx.shape
    gw = 2 * bc_pre.shape[2]
    heads = dt_t.shape[0]
    n_state = gw // 2
    nt = t // q
    width = inner + gw
    full = lambda shape: pl.BlockSpec(shape, lambda c: (0,) * len(shape))
    return pl.pallas_call(
        functools.partial(phase_a_kernel, q, heads, inner, gw),
        grid=(nt,),
        in_specs=[pl.BlockSpec((1, q, inner), lambda c: (1, c, 0)), pl.BlockSpec((2, q, gw // 2), lambda c: (0, c, 0)),
                  pl.BlockSpec((heads, q), lambda c: (0, c)), pl.BlockSpec((1, q), lambda c: (0, c)),
                  full((8, inner)), full((2, 8, gw // 2)), full((1, 128)), full((4, width)), full((1, width)), full((heads, 1)), full((heads, 1))],
        out_specs=[pl.BlockSpec((q, inner), lambda c: (c, 0)), pl.BlockSpec((q, gw), lambda c: (c, 0)),
                   pl.BlockSpec((heads, q), lambda c: (0, c)), pl.BlockSpec((heads, q), lambda c: (0, c)),
                   pl.BlockSpec((1, n_state, inner), lambda c: (c, 0, 0)), full((n_state, inner)), full((1, inner))],
        out_shape=[jax.ShapeDtypeStruct((t, inner), BF16), jax.ShapeDtypeStruct((t, gw), BF16),
                   jax.ShapeDtypeStruct((heads, t), F32), jax.ShapeDtypeStruct((heads, t), F32),
                   jax.ShapeDtypeStruct((nt, n_state, inner), F32), jax.ShapeDtypeStruct((n_state, inner), F32),
                   jax.ShapeDtypeStruct((1, inner), F32)],
        scratch_shapes=[pltpu.VMEM((q + 8, width), F32), pltpu.VMEM((q, inner), BF16), pltpu.VMEM((n_state, inner), F32), pltpu.VMEM((1, 128), F32)],
        compiler_params=pltpu.CompilerParams(dimension_semantics=("arbitrary",), vmem_limit_bytes=48 * 2**20),
        cost_estimate=pl.CostEstimate(flops=20 * 10**9, bytes_accessed=40 * 2**20, transcendentals=0),
        name="phase_a",
    )(zx, bc_pre, dt_t, seg_row, tail_x, tail_bc, tail_seg, conv_w, conv_b, neg_a, dt_bias)


def phase_b_kernel(q, heads, inner, gw, xact_ref, bc_ref, cum_ref, cl_ref, seg_ref, sloc_ref, sin_ref, z_ref, dskip_ref, nw_ref,
                   out_ref, pd, sbf, yoff, gated, segprev):
    c = pl.program_id(0)
    head_dim = inner // heads
    n_state = gw // 2
    half = q // 2

    @pl.when(c == 0)
    def _():
        pd[...] = jnp.ones_like(pd)
        segprev[...] = jnp.zeros_like(segprev)

    seg_row = seg_ref[...]
    seg_prev = segprev[:, 127:128]
    segprev[...] = seg_row[:, q - 128:]
    seg_last = seg_row[:, q - 1:q]
    seg_rows = jnp.broadcast_to(seg_row, (q, q))
    seg_cols = seg_rows.T
    causal = lax.broadcasted_iota(jnp.int32, (q, q), 0) >= lax.broadcasted_iota(jnp.int32, (q, q), 1)
    bias = jnp.where(causal & (seg_rows == seg_cols), 0.0, NEG)
    cum = cum_ref[...]
    cl = cl_ref[...]
    cum_cols = cum.T
    keep_in = jnp.where(seg_row == seg_prev, jnp.exp2(cum), 0.0)
    in_cols = keep_in.T
    carry = jnp.where(seg_last == seg_prev, jnp.exp2(cum[:, q - 1:q]), 0.0)
    carry_lane = expand_heads(jnp.broadcast_to(carry, (heads, 128)).T[0:8, :], head_dim)[0:1, :]
    sbf[...] = (sloc_ref[0] + pd[...] * sin_ref[...]).astype(BF16)
    pd[...] = pd[...] * carry_lane
    b_act = bc_ref[:, 0:n_state]
    c_act = bc_ref[:, n_state:gw]
    scores = lax.dot_general(c_act, b_act, (((1,), (1,)), ((), ())), preferred_element_type=F32)
    yoff[...] = jnp.dot(c_act, sbf[...], preferred_element_type=F32)
    lane = lax.broadcasted_iota(jnp.int32, (q, 128), 1)
    per = 128 // head_dim
    sq = jnp.zeros((q, 128), F32)
    for i in range(inner // 128):
        cols = slice(i * 128, (i + 1) * 128)
        x_b = xact_ref[:, cols]
        x_f = x_b.astype(F32)
        y_top = jnp.zeros((half, 128), F32)
        y_bot = jnp.zeros((half, 128), F32)
        for j in range(per):
            h = i * per + j
            x_h = jnp.where((lane >= j * head_dim) & (lane < (j + 1) * head_dim), x_f, 0.0).astype(BF16)
            ccol = cum_cols[:, h:h + 1]
            crow = cl[h:h + 1, :]
            m_top = jnp.exp2(ccol[0:half] + bias[0:half, 0:half] - crow[:, 0:half]) * scores[0:half, 0:half]
            m_bot = jnp.exp2(ccol[half:q] + bias[half:q, :] - crow) * scores[half:q, :]
            y_top = y_top + jnp.dot(m_top.astype(BF16), x_h[0:half], preferred_element_type=F32)
            y_bot = y_bot + jnp.dot(m_bot.astype(BF16), x_h, preferred_element_type=F32)
        y = jnp.concatenate([y_top, y_bot], axis=0)
        y = y + yoff[:, cols] * head_lanes(in_cols, i, head_dim, q)
        y = y + dskip_ref[0:1, cols] * x_f
        v = y * silu(z_ref[0, :, cols].astype(F32))
        gated[:, cols] = v
        sq = sq + v * v
    inv = lax.rsqrt(jnp.sum(sq, axis=1, keepdims=True) * (1.0 / inner) + NORM_EPS)
    inv = jnp.broadcast_to(inv, (q, 128))
    for i in range(inner // 128):
        cols = slice(i * 128, (i + 1) * 128)
        out_ref[:, cols] = (gated[:, cols] * inv * nw_ref[0:1, cols]).astype(BF16)


def phase_b(x_act, bc_act, cum, cl, seg_row, sloc, s_in, z_arr, dskip_lane, norm_w, q=256):
    t, inner = x_act.shape
    gw = bc_act.shape[1]
    heads = cum.shape[0]
    n_state = gw // 2
    nt = t // q
    full = lambda shape: pl.BlockSpec(shape, lambda c: (0,) * len(shape))
    return pl.pallas_call(
        functools.partial(phase_b_kernel, q, heads, inner, gw),
        grid=(nt,),
        in_specs=[pl.BlockSpec((q, inner), lambda c: (c, 0)), pl.BlockSpec((q, gw), lambda c: (c, 0)),
                  pl.BlockSpec((heads, q), lambda c: (0, c)), pl.BlockSpec((heads, q), lambda c: (0, c)),
                  pl.BlockSpec((1, q), lambda c: (0, c)), pl.BlockSpec((1, n_state, inner), lambda c: (c, 0, 0)),
                  full((n_state, inner)), pl.BlockSpec((1, q, inner), lambda c: (0, c, 0)), full((1, inner)), full((1, inner))],
        out_specs=pl.BlockSpec((q, inner), lambda c: (c, 0)),
        out_shape=jax.ShapeDtypeStruct((t, inner), BF16),
        scratch_shapes=[pltpu.VMEM((1, inner), F32), pltpu.VMEM((n_state, inner), BF16), pltpu.VMEM((q, inner), F32), pltpu.VMEM((q, inner), F32), pltpu.VMEM((1, 128), F32)],
        compiler_params=pltpu.CompilerParams(dimension_semantics=("arbitrary",), vmem_limit_bytes=48 * 2**20),
        cost_estimate=pl.CostEstimate(flops=20 * 10**9, bytes_accessed=40 * 2**20, transcendentals=0),
        name="phase_b",
    )(x_act, bc_act, cum, cl, seg_row, sloc, s_in, z_arr, dskip_lane, norm_w)


def out_kernel(chips, nb, wc, slots, v_ref, wo_ref, wp_ref, x_ref, o_ref,
               va_own, va_par, wbuf, send, recv, xo,
               vo_sem, vs_sem, vr_sem, w_sem, s_sem, r_sem, x_sem, o_sem):
    me = lax.axis_index('tp')
    chip = me // 2
    core = lax.rem(me, 2)
    partner = 2 * chip + 1 - core
    right = 2 * lax.rem(chip + 1, chips) + core
    left = 2 * lax.rem(chip + chips - 1, chips) + core
    rows = va_own.shape[1]
    half = nb * wc
    steps = chips * nb * 2

    barrier = pltpu.get_barrier_semaphore()
    for peer in (partner, left, right):
        pl.semaphore_signal(barrier, inc=1, device_id={'tp': peer}, device_id_type=MESH)

    def cols_of(u):
        return pl.multiple_of(lax.rem(u, 2) * half + lax.rem(u // 2, nb) * wc, wc)

    def w_copies(u, slot):
        col = cols_of(u)
        return (pltpu.make_async_copy(wo_ref.at[:, pl.ds(col, wc)], wbuf.at[slot, 0], w_sem.at[slot, 0]),
                pltpu.make_async_copy(wp_ref.at[:, pl.ds(col, wc)], wbuf.at[slot, 1], w_sem.at[slot, 1]))

    for cp in w_copies(0, 0):
        cp.start()
    x_copy = pltpu.make_async_copy(x_ref, xo, x_sem)
    order = [lax.rem(chip + d, chips) for d in (chips - 1, 1, 2, 0)]

    def own_copy(j):
        return pltpu.make_async_copy(v_ref.at[pl.ds(pl.multiple_of((2 * j + core) * rows, rows), rows), :], va_own.at[j], vo_sem.at[j])

    def par_copy(j):
        return pltpu.make_async_remote_copy(
            src_ref=v_ref.at[pl.ds(pl.multiple_of((2 * j + 1 - core) * rows, rows), rows), :], dst_ref=va_par.at[j],
            send_sem=vs_sem.at[j], recv_sem=vr_sem.at[j], device_id={'tp': partner}, device_id_type=MESH)

    for j in order:
        own_copy(j).start()
    pl.semaphore_wait(barrier, 3)
    for j in order:
        par_copy(j).start()
    x_copy.start()
    for j in order:
        own_copy(j).wait()

    def ring_copy(d, unit):
        slot = lax.rem(unit, slots)
        return pltpu.make_async_remote_copy(
            src_ref=send.at[d, slot], dst_ref=recv.at[d, unit], send_sem=s_sem.at[d, slot], recv_sem=r_sem.at[d, unit],
            device_id={'tp': jnp.where(d == 0, right, left)}, device_id_type=MESH)

    def body(u, carry):
        d = lax.rem(u, 2)
        k = u // (2 * nb)
        b = lax.rem(u // 2, nb)
        slot = lax.rem(u, 2)
        unit = k * nb + b
        dest = lax.rem(jnp.where(d == 0, chip + 2 * chips - 1 - k, chip + 1 + k), chips)
        for cp in w_copies(u, slot):
            cp.wait()

        @pl.when(u + 1 < steps)
        def _():
            for cp in w_copies(u + 1, 1 - slot):
                cp.start()

        @pl.when((b == 0) & ((k == 0) | ((d == 0) & ((k == 1) | (k == 3)))))
        def _():
            par_copy(dest).wait_recv()

        part = jnp.dot(va_own[dest], wbuf[slot, 0], preferred_element_type=F32)
        part = part + jnp.dot(va_par[dest], wbuf[slot, 1], preferred_element_type=F32)

        @pl.when(k < chips - 1)
        def _():
            sslot = lax.rem(unit, slots)

            @pl.when(unit >= slots)
            def _():
                ring_copy(d, unit - slots).wait_send()

            @pl.when(k == 0)
            def _():
                send[d, sslot] = part

            @pl.when(k > 0)
            def _():
                ring_copy(d, unit - nb).wait_recv()
                send[d, sslot] = part + recv[d, unit - nb]
            ring_copy(d, unit).start()

        @pl.when(k == chips - 1)
        def _():
            @pl.when((b == 0) & (d == 0))
            def _():
                x_copy.wait()
            ring_copy(d, unit - nb).wait_recv()
            cols = pl.ds(cols_of(u), wc)
            xo[:, cols] = (xo[:, cols].astype(F32) + (part + recv[d, unit - nb])).astype(BF16)
            pltpu.make_async_copy(xo.at[:, cols], o_ref.at[:, cols], o_sem.at[d, b]).start()
        return carry

    lax.fori_loop(0, steps, body, 0)

    def drain_out(u, carry):
        d = lax.rem(u, 2)
        b = u // 2
        cols = pl.ds(pl.multiple_of(d * half + b * wc, wc), wc)
        pltpu.make_async_copy(xo.at[:, cols], o_ref.at[:, cols], o_sem.at[d, b]).wait()
        return carry

    def drain_send(u, carry):
        ring_copy(lax.rem(u, 2), (chips - 1) * nb - slots + u // 2).wait_send()
        return carry

    lax.fori_loop(0, 2 * slots, drain_send, 0)
    for j in order:
        par_copy(j).wait_send()
    lax.fori_loop(0, 2 * nb, drain_out, 0)


def out_proj_scatter(v, w_own, w_par, x_loc, chips, wc=512, slots=4):
    t, inner = v.shape
    rows, d_model = x_loc.shape
    nb = d_model // 2 // wc
    any_spec = pl.BlockSpec(memory_space=pl.ANY)
    dma = pltpu.SemaphoreType.DMA
    return pl.pallas_call(
        functools.partial(out_kernel, chips, nb, wc, slots),
        in_specs=[any_spec] * 4,
        out_specs=any_spec,
        out_shape=jax.ShapeDtypeStruct((rows, d_model), BF16),
        scratch_shapes=[pltpu.VMEM((chips, rows, inner), BF16), pltpu.VMEM((chips, rows, inner), BF16), pltpu.VMEM((2, 2, inner, wc), BF16),
                        pltpu.VMEM((2, slots, rows, wc), F32), pltpu.VMEM((2, (chips - 1) * nb, rows, wc), F32), pltpu.VMEM((rows, d_model), BF16),
                        dma((chips,)), dma((chips,)), dma((chips,)), dma((2, 2)), dma((2, slots)), dma((2, (chips - 1) * nb)), dma, dma((2, nb))],
        compiler_params=pltpu.CompilerParams(collective_id=1, has_side_effects=True, vmem_limit_bytes=60 * 2**20),
        cost_estimate=pl.CostEstimate(flops=2 * t * inner * d_model, bytes_accessed=300 * 2**20, transcendentals=0),
        name="out_proj_scatter",
    )(v, w_own, w_par, x_loc)


def chain_state(end_state, block_decay, seq_axis, n_blocks):
    dev_index = lax.axis_index(seq_axis)
    to_next = [(src_dev, src_dev + 1) for src_dev in range(n_blocks - 1)]
    state_in = lax.ppermute(end_state, seq_axis, to_next)
    decay_in = jnp.where(dev_index == 0, 1.0, lax.ppermute(block_decay, seq_axis, to_next))
    for step_idx in range((n_blocks - 1).bit_length()):
        hop_span = 2 ** step_idx
        hop_perm = [(src_dev, src_dev + hop_span) for src_dev in range(n_blocks - hop_span)]
        prev_state = lax.ppermute(state_in, seq_axis, hop_perm)
        prev_decay = lax.ppermute(decay_in, seq_axis, hop_perm)
        has_prev = dev_index >= hop_span
        state_in = jnp.where(has_prev, decay_in * prev_state + state_in, state_in)
        decay_in = jnp.where(has_prev, decay_in * prev_decay, decay_in)
    return state_in


def local_layer(x_loc, x_blk, seg_blk, w_out_par, weights, n_blocks, chips):
    w_zx, w_bc, w_dt, conv_x, conv_bc, bias_x, bias_bc, a_log, dt_bias, d_skip, norm_w, w_out = weights
    t = x_blk.shape[0]
    inner = w_zx.shape[2]
    n_state = w_bc.shape[2]
    heads = w_dt.shape[1]
    head_dim = inner // heads
    zx = jnp.einsum('ld,dkc->klc', x_blk, w_zx, preferred_element_type=F32).astype(BF16)
    bc_pre = jnp.einsum('ld,dkc->klc', x_blk, w_bc, preferred_element_type=F32).astype(BF16)
    dt_t = jnp.einsum('ld,dh->hl', x_blk, w_dt, preferred_element_type=F32).astype(BF16)
    to_next = [(src, src + 1) for src in range(n_blocks - 1)]
    tail_x = lax.ppermute(zx[1, t - 8:], 'sp', to_next)
    tail_bc = lax.ppermute(bc_pre[:, t - 8:], 'sp', to_next)
    tail_seg = lax.ppermute(seg_blk[t - 8:], 'sp', to_next)
    seg_prev = jnp.where(lax.axis_index('sp') == 0, seg_blk[0], tail_seg[7])
    seg_row = (seg_blk - seg_prev).astype(F32)[None]
    tail_row = jnp.pad((tail_seg - seg_prev).astype(F32), (120, 0), constant_values=-1e6)[None]
    conv_w = jnp.concatenate([conv_x, conv_bc.reshape(conv_bc.shape[0], 2 * n_state)], axis=1).astype(F32)
    conv_b = jnp.concatenate([bias_x, bias_bc.reshape(2 * n_state)]).astype(F32)[None]
    x_act, bc_act, cum, cl, sloc, s_end, dec = phase_a(zx, bc_pre, dt_t, seg_row, tail_x, tail_bc, tail_row, conv_w, conv_b, -jnp.exp(a_log)[:, None], dt_bias[:, None])
    s_in = chain_state(s_end, dec, 'sp', n_blocks)
    v = phase_b(x_act, bc_act, cum, cl, seg_row, sloc, s_in, zx, jnp.repeat(d_skip, head_dim)[None], norm_w.astype(F32)[None])
    return out_proj_scatter(v, w_out, w_out_par, x_loc, chips)


def solution(mesh):
    n_blocks = mesh.shape['sp']
    n_tp = mesh.shape['tp']
    token_spec = P(('dp', 'sp', 'tp'), None)
    seg_spec = P(('dp', 'sp', 'tp'))
    weight_specs = (P(None, None, 'tp'), P(None, None, 'tp'), P(None, 'tp'), P(None, 'tp'), P(None, None, 'tp'), P('tp'), P(None, 'tp'), P('tp'), P('tp'), P('tp'), P('tp'), P('tp', None))

    def body(x_loc, seg_loc, *weights):
        w_out_par = lax.ppermute(weights[-1], 'tp', [(i, i ^ 1) for i in range(n_tp)])
        x_blk = lax.all_gather(x_loc, 'tp', axis=0, tiled=True)
        seg_blk = lax.all_gather(seg_loc, 'tp', axis=0, tiled=True)
        return local_layer(x_loc, x_blk, seg_blk, w_out_par, weights, n_blocks, n_tp // 2)

    return jax.shard_map(body, mesh=mesh, in_specs=(token_spec, seg_spec) + weight_specs, out_specs=token_spec, check_vma=False)
```

time: 1570 us -> 800 us (0.51)
  local copies, waits for them, and re-layouts: 532 us -> 9.73 us
  Pallas kernels: 0 us -> 349 us
  waiting for transfers between devices: 492 us -> 183 us
  matrix products: 357 us -> 185 us
  other arithmetic: 99.5 us -> 4.5 us
    dynamic_update_slice x16 -> x0, local copies, waits for them, and re-layouts: 396 us -> none  [block_ssd(): end_state, y_tiles = lax.scan(body, init_state, tiles_in)]
    pallas_call x0 -> x3, Pallas kernels: none -> 349 us  [the longest x1 284 us: out_proj_scatter(): pl.pallas_call(functools.partial(out_kernel, chips, nb, wc, slots), in_sp...]
    reduce_scatter x1 -> x0, waiting for transfers between devices: 328 us -> none  [body(): out_loc = lax.psum_scatter(out_part, 'tp', scatter_dimension=0, tiled=True)]
    dot_general x37 -> x3, matrix products: 357 us -> 185 us  [the longest x1 154 us: local_layer(): jnp.einsum('ld,dkc->klc', x_blk, w_zx, preferred_element_type=F32)]
    convert_element_type x7 -> x4, other arithmetic: 41.1 us -> 0.75 us  [the longest x1 0.73 us: local_layer(): jnp.concatenate([conv_x, conv_bc.reshape(conv_bc.shape[0], 2 * n_state)],...]
    reshape x12 -> x0, local copies, waits for them, and re-layouts: 36.2 us -> none  [the longest x1 18.1 us: block_ssd(): return (end_state, y_tiles.reshape(row_count, groups, per_group, head_dim))]
    another operation x40 -> x1, local copies, waits for them, and re-layouts: 27.1 us -> 0.08 us  [local_layer(): jnp.repeat(d_skip, head_dim)[None]]
    slice x31 -> x4, local copies, waits for them, and re-layouts: 20.2 us -> 1.22 us  [the longest x2 1.15 us: local_layer(): seg_prev = jnp.where(lax.axis_index('sp') == 0, seg_blk[0], tail_seg[7])]
  transfers between devices with their start and end apart: 10 -> 10, of which waited for: 5 -> 4; matrix products, arithmetic and copies ran while one was open for 15% -> 24% of each run, Pallas kernels for 0% -> 8%
where the time goes in v1:
time: 800 us; the launch traced here: 799 us
  Pallas kernels  349 us (44%)
  matrix products  185 us (23%)
  waiting for transfers between devices  183 us (23%)
  starting transfers between devices  34.3 us (4%)
  blocking collectives  18.9 us (2%)
  between operations  14.9 us (2%)
  local copies, waits for them, and re-layouts  9.73 us (1%)
    pallas_call x1, Pallas kernels, out_proj_scatter(): pl.pallas_call(functools.partial(out_kernel, chips, nb, wc, slots), in_sp...  284 us
    dot_general x1, matrix products, local_layer(): jnp.einsum('ld,dkc->klc', x_blk, w_zx, preferred_element_type=F32)  154 us
    all_gather x1, waiting for transfers between devices, body(): x_blk = lax.all_gather(x_loc, 'tp', axis=0, tiled=True)  124 us
    pallas_call x1, Pallas kernels, phase_b(): pl.pallas_call(functools.partial(phase_b_kernel, q, heads, inner, gw), gr...  33.2 us
    pallas_call x1, Pallas kernels, phase_a(): pl.pallas_call(functools.partial(phase_a_kernel, q, heads, inner, gw), gr...  31.9 us
    ppermute x1, waiting for transfers between devices, chain_state(): state_in = lax.ppermute(end_state, seq_axis, to_next)  21.6 us
    all_gather x1, blocking collectives, body(): seg_blk = lax.all_gather(seg_loc, 'tp', axis=0, tiled=True)  18.9 us
    ppermute x1, waiting for transfers between devices, chain_state(): lax.ppermute(block_decay, seq_axis, to_next)  18.7 us
  transfers between devices with their start and end apart: 10, of which 4 were waited for; matrix products, arithmetic and copies ran while one was open for 24% of the time, Pallas kernels for 8%

profile of v1, /device:TPU:97, one launch (start us, length us, event | category | flops | bytes accessed | tf_op | source)
XLA Modules:
  0.0 798.8 jit_solution(14551520617895733152)
XLA Ops:
  6.5 0.0 copy-start
  6.6 0.7 all-gather.3.cloned.1.call-update
  7.3 18.9 %all-gather = s32[8,1,256]{2,1,0:T(1,128)S(1)} all-gather(s32[1,1,256]{2,1,0:T(1,128)} %bitcast.51), channel_id=1, replica_groups=mesh['dp'=1,'sp'=4,'tp'=8] {'tp'}, dimensions={0}, use_global_device_ids=true | all-gather | bytes 9216 | tf_op jit(solution)/shard_map/all_gather | solution.py:416
  26.2 0.1 slice.21
  26.2 3.8 collective-permute-start
  30.0 6.5 collective-permute-start.8
  36.5 0.5 slice.20
  37.0 0.7 copy.40
  37.7 0.7 copy.41
  38.4 0.7 concatenate.18
  39.1 0.7 negate_bitcast_fusion
  39.7 0.1 copy.23.alog_ref
  39.8 0.7 copy.24.dtb_ref
  40.6 0.7 maximum_convert_fusion.cw_ref
  41.3 0.0 collective-permute-done
  41.3 0.6 slice.17
  43.2 0.1 pad_bitcast_fusion.tailseg_ref
  43.3 124.2 %all-gather.3.cloned.1.call-done = bf16[2048,8192]{1,0:T(8,128)(2,1)} async-done(((bf16[256,8192]{1,0:T(8,128)(2,1)}), bf16[2048,8192]{1,0:T(8,128)(2,1)}) %all-gather.3.cloned.1.call-update) | async-done | bytes 33554448 | tf_op jit(solution)/shard_map/all_gather | solution.py:415
  167.5 153.9 %convert_bitcast_fusion.x_ref.z_ref = bf16[2,2048,2048]{2,1,0:T(8,128)(2,1)} fusion(bf16[8192,2,2048]{2,1,0:T(2,128)(2,1)} %param.16, bf16[2048,8192]{1,0:T(8,128)(2,1)} %all-gather.3.cloned.1.call-done), kind=kOutput, calls=%fused_computation.5 | convolution fusion | flops 137447342080 | bytes 117440512 | tf_op jit(solution)/shard_map/ld,dkc->klc/dot_general | solution.py:388
  321.5 0.8 slice_bitcast_fusion
  322.2 3.3 collective-permute-start.1
  325.6 16.3 %fusion.15.bc_ref = bf16[2,2048,128]{2,1,0:T(8,128)(2,1)S(1)} fusion(bf16[8192,2,128]{2,1,0:T(2,128)(2,1)} %param.17, bf16[2048,8192]{1,0:T(8,128)(2,1)} %all-gather.3.cloned.1.call-done), kind=kOutput, calls=%fused_computation.8 | convolution fusion | flops 8590458880 | bytes 38797312 | tf_op jit(solution)/shard_map/ld,dkc->klc/dot_general | solution.py:389
  341.9 3.2 collective-permute-start.2
  345.0 0.0 copy-done
  345.0 15.2 %convolution_convert_fusion.dt_ref = bf16[32,2048]{1,0:T(8,128)(2,1)S(1)} fusion(bf16[8192,32]{0,1:T(8,128)(2,1)S(1)} %copy-done, bf16[2048,8192]{1,0:T(8,128)(2,1)} %all-gather.3.cloned.1.call-done), kind=kOutput, calls=%fused_computation.9 | convolution fusion | flops 1073807360 | bytes 34209792 | tf_op jit(solution)/shard_map/ld,dh->hl/dot_general | solution.py:390
  360.2 0.0 collective-permute-done.2.tailbc_ref
  360.2 0.0 collective-permute-done.1.tailx_ref
  360.2 0.0 copy-start.3
  360.3 0.0 copy-start.2
  360.3 31.9 %phase_a.1 = (bf16[2048,2048]{1,0:T(8,128)(2,1)}, bf16[2048,256]{1,0:T(8,128)(2,1)S(1)}, f32[32,2048]{1,0:T(8,128)S(1)}, f32[32,2048]{1,0:T(8,128)S(1)}, f32[8,1...) custom-call(bf16[2,2048,2048]{2,1,0:T(8,128)(2,1)} %convert_bitcast_fusion.x_ref.z_ref, ...), custom_call_target="tpu_custom_call" | custom-call | flops 20000000000 | bytes 41943040 | tf_op jit(solution)/shard_map/phase_a/pallas_call | solution.py:115
  392.2 2.9 collective-permute-start.5
  395.1 21.6 %collective-permute-done.5 = f32[128,2048]{1,0:T(8,128)S(1)} collective-permute-done((f32[128,2048]{1,0:T(8,128)S(1)}, f32[128,2048]{1,0:T(8,128)S(1)}, u32[]{:S(2)}, u32[]{:S(2)}) %collective-permute-start.5) | collective-permute-done | bytes 1048608 | tf_op jit(solution)/shard_map/ppermute | solution.py:368
  416.7 5.1 collective-permute-start.6
  421.8 1.3 collective-permute-start.3
  423.1 18.7 %collective-permute-done.3 = f32[1,2048]{1,0:T(1,128)S(1)} collective-permute-done((f32[1,2048]{1,0:T(1,128)S(1)}, f32[1,2048]{1,0:T(1,128)S(1)}, u32[]{:S(2)}, u32[]{:S(2)}) %collective-permute-start.3) | collective-permute-done | bytes 8224 | tf_op jit(solution)/shard_map/ppermute | solution.py:369
  441.8 0.0 collective-permute-done.6
  441.9 1.7 add_select_fusion.1
  443.6 6.1 collective-permute-start.7
  449.7 2.1 collective-permute-start.4
  451.8 0.1 broadcast_in_dim.27
  451.9 0.1 broadcast_in_dim_reshape.3.dskip_ref
  452.0 17.2 %collective-permute-done.4 = f32[1,2048]{1,0:T(1,128)S(1)} collective-permute-done((f32[1,2048]{1,0:T(1,128)S(1)}, f32[1,2048]{1,0:T(1,128)S(1)}, u32[]{:S(2)}, u32[]{:S(2)}) %collective-permute-start.4) | collective-permute-done | bytes 8224 | tf_op jit(solution)/shard_map/ppermute | solution.py:374
  469.2 0.0 collective-permute-done.7
  469.3 1.4 add_select_fusion.sin_ref
  470.6 33.2 %phase_b.1.v_ref = bf16[2048,2048]{1,0:T(8,128)(2,1)} custom-call(bf16[2048,2048]{1,0:T(8,128)(2,1)} %get-tuple-element.12.xact_ref, bf16[2048,256]{1,0:T(8,128)(2,1)S(1)} %get-tuple-element.13.bc_ref, f32[32,2048]{1,0:T(8,128)S(1)} %get-tuple-element.14.cum_ref, f32[32,2048]{1,0:T(8,128)S(1)} %get-tuple-element.15.cl_ref, f32[1,2048]{1,0:T(1,128)S(1)} %bitcast.43, ...), custom_call_target="tpu_custom_call" | custom-call | flops 20000000000 | bytes 41943040 | tf_op jit(solution)/shard_map/phase_b/pallas_call | solution.py:206
  503.8 0.0 collective-permute-done.8.wp_ref
  503.8 283.5 %out_proj_scatter.1 = bf16[256,8192]{1,0:T(8,128)(2,1)} custom-call(bf16[2048,2048]{1,0:T(8,128)(2,1)} %phase_b.1.v_ref, bf16[2048,8192]{1,0:T(8,128)(2,1)} %wo_ref.1, bf16[2048,8192]{1,0:T(8,128)(2,1)} %collective-permute-done.8.wp_ref, bf16[256,8192]{1,0:T(8,128)(2,1)} %x_ref.1), custom_call_target="tpu_custom_call" | custom-call | flops 68719476736 | bytes 314572800 | tf_op jit(solution)/shard_map/out_proj_scatter/pallas_call | solution.py:351
  787.3 4.6 copy.43
  (12 shorter events, 0.1 us)
Async XLA Ops:
  6.5 338.5 %copy-start = (bf16[8192,32]{0,1:T(8,128)(2,1)S(1)}, bf16[8192,32]{0,1:T(8,128)(2,1)}, u32[]{:S(2)}) copy-start(bf16[8192,32]{0,1:T(8,128)(2,1)} %param.18) | copy-start | bytes 1572868
  6.6 161.0 %all-gather.3.cloned.1.call-start = ((), (), s32[]{:S(2)}) async-start(), calls=%async_computation | async-start | bytes 37748736 | tf_op jit(solution)/shard_map/all_gather | solution.py:415
  26.2 15.1 %collective-permute-start = (s32[8]{0:T(128)S(1)}, s32[8]{0:T(128)S(1)}, u32[]{:S(2)}, u32[]{:S(2)}) collective-permute-start(s32[8]{0:T(128)S(1)} %slice.21), channel_id=1, source_target_pairs={{0,8},{8,16},{16,24},{1,9},{9,17},{17,25},{2,10},{10,18},{18,26},{... | collective-permute-start | bytes 104 | tf_op jit(solution)/shard_map/ppermute | solution.py:394
  30.0 473.8 %collective-permute-start.8 = (bf16[2048,8192]{1,0:T(8,128)(2,1)}, bf16[2048,8192]{1,0:T(8,128)(2,1)}, u32[]{:S(2)}, u32[]{:S(2)}) collective-permute-start(bf16[2048,8192]{1,0:T(8,128)(2,1)} %wo_ref.1), channel_id=1, source_target_pairs={{0,1},{1,0},{2,3},{3,2},{4,5},{5,4},{6,7},{7,6},{8,9},{9,8},{10,11... | collective-permute-start | bytes 100663304 | tf_op jit(solution)/shard_map/ppermute | solution.py:414
  322.2 38.0 %collective-permute-start.1 = (bf16[8,2048]{1,0:T(8,128)(2,1)S(1)}, bf16[8,2048]{1,0:T(8,128)(2,1)S(1)}, u32[]{:S(2)}, u32[]{:S(2)}) collective-permute-start(bf16[8,2048]{1,0:T(8,128)(2,1)S(1)} %slice_bitcast_fusion), channel_id=1, source_target_pairs={{0,8},{8,16},{16,24},{1,9},{9,17},{17,25},{2,10},{10,18},{18,26},{... | collective-permute-start | bytes 98312 | tf_op jit(solution)/shard_map/ppermute | solution.py:392
  341.9 18.4 %collective-permute-start.2 = (bf16[2,8,128]{2,1,0:T(8,128)(2,1)S(1)}, bf16[2,8,128]{2,1,0:T(8,128)(2,1)S(1)}, u32[]{:S(2)}, u32[]{:S(2)}) collective-permute-start(bf16[2,8,128]{2,1,0:T(8,128)(2,1)S(1)} %slice.23), channel_id=1, source_target_pairs={{0,8},{8,16},{16,24},{1,9},{9,17},{17,25},{2,10},{10,18},{18,26},{... | collective-permute-start | bytes 12296 | tf_op jit(solution)/shard_map/ppermute | solution.py:393
  360.2 91.6 %copy-start.3 = (f32[32]{0:T(128)S(1)}, f32[32]{0:T(128)}, u32[]{:S(2)}) copy-start(f32[32]{0:T(128)} %param.25) | copy-start | bytes 388
  360.3 91.7 %copy-start.2 = (bf16[2048]{0:T(1024)(128)(2,1)S(1)}, bf16[2048]{0:T(1024)(128)(2,1)}, u32[]{:S(2)}) copy-start(bf16[2048]{0:T(1024)(128)(2,1)} %param.26) | copy-start | bytes 12292
  392.2 24.5 %collective-permute-start.5 = (f32[128,2048]{1,0:T(8,128)S(1)}, f32[128,2048]{1,0:T(8,128)S(1)}, u32[]{:S(2)}, u32[]{:S(2)}) collective-permute-start(f32[128,2048]{1,0:T(8,128)S(1)} %get-tuple-element.18), channel_id=1, source_target_pairs={{0,8},{8,16},{16,24},{1,9},{9,17},{17,25},{2,10},{10,18},{18,26},{... | collective-permute-start | bytes 3145736 | tf_op jit(solution)/shard_map/ppermute | solution.py:368
  416.7 25.2 %copy-start.1 = (f32[128,2048]{1,0:T(8,128)}, f32[128,2048]{1,0:T(8,128)S(1)}, u32[]{:S(2)}) copy-start(f32[128,2048]{1,0:T(8,128)S(1)} %collective-permute-done.5) | copy-start | bytes 3145732
  416.7 25.1 %collective-permute-start.6 = (f32[128,2048]{1,0:T(8,128)S(1)}, f32[128,2048]{1,0:T(8,128)}, u32[]{:S(2)}, u32[]{:S(2)}) collective-permute-start(f32[128,2048]{1,0:T(8,128)S(1)} %collective-permute-done.5), channel_id=1, source_target_pairs={{0,8},{8,16},{16,24},{1,9},{9,17},{17,25},{2,10},{10,18},{18,26},{... | collective-permute-start | bytes 3145736 | tf_op jit(solution)/shard_map/ppermute | solution.py:373
  421.8 20.0 %collective-permute-start.3 = (f32[1,2048]{1,0:T(1,128)S(1)}, f32[1,2048]{1,0:T(1,128)S(1)}, u32[]{:S(2)}, u32[]{:S(2)}) collective-permute-start(f32[1,2048]{1,0:T(1,128)S(1)} %get-tuple-element.17), channel_id=1, source_target_pairs={{0,8},{8,16},{16,24},{1,9},{9,17},{17,25},{2,10},{10,18},{18,26},{... | collective-permute-start | bytes 24584 | tf_op jit(solution)/shard_map/ppermute | solution.py:369
  443.6 25.7 %collective-permute-start.7 = (f32[128,2048]{1,0:T(8,128)S(1)}, f32[128,2048]{1,0:T(8,128)}, u32[]{:S(2)}, u32[]{:S(2)}) collective-permute-start(f32[128,2048]{1,0:T(8,128)S(1)} %add_select_fusion.1), channel_id=1, source_target_pairs={{0,16},{8,24},{1,17},{9,25},{2,18},{10,26},{3,19},{11,27},{4,20},{... | collective-permute-start | bytes 3145736 | tf_op jit(solution)/shard_map/ppermute | solution.py:373
  449.7 19.5 %collective-permute-start.4 = (f32[1,2048]{1,0:T(1,128)S(1)}, f32[1,2048]{1,0:T(1,128)S(1)}, u32[]{:S(2)}, u32[]{:S(2)}) collective-permute-start(f32[1,2048]{1,0:T(1,128)S(1)} %broadcast_select_fusion), channel_id=1, source_target_pairs={{0,8},{8,16},{16,24},{1,9},{9,17},{17,25},{2,10},{10,18},{18,26},{... | collective-permute-start | bytes 24584 | tf_op jit(solution)/shard_map/ppermute | solution.py:374
Sparse Core Ops, SparseCore 0:
  9.0 158.5 all-gather.2

commit v2 on v0

v2 whole, which is shorter than its diff:
```python
import functools
import jax
import jax.numpy as jnp
from jax import lax
from jax.experimental import pallas as pl
from jax.experimental.pallas import tpu as pltpu
from jax.sharding import PartitionSpec as P

MESH = pl.DeviceIdType.MESH
NORM_EPS = 1e-5
LOG2E = 1.4426950408889634
FAR = -1e6
NEG = -1e30
F32 = jnp.float32
BF16 = jnp.bfloat16
HI = lax.Precision.HIGHEST
MIB = 2 ** 20
LANES = 128
ROW8 = 8
CORES = 2
PAIR = range(2)
ANY = pl.BlockSpec(memory_space=pl.ANY)
VMEM = pl.BlockSpec(memory_space=pltpu.VMEM)
DMA = pltpu.SemaphoreType.DMA


def scratch(dtype, *shape):
    return pltpu.VMEM(shape, dtype)


def out_of(dtype, *shape):
    return jax.ShapeDtypeStruct(shape, dtype)


def sems(*shape):
    return DMA(shape)


def rows_at(start, size):
    return pl.ds(pl.multiple_of(start, size), size)


def odd(i):
    return lax.rem(i, 2)


def flip(i):
    return 1 - i


def dot32(a, b):
    return jnp.dot(a, b, preferred_element_type=F32)


def params(limit, name_id=None):
    if name_id is None:
        return pltpu.CompilerParams(dimension_semantics=('arbitrary',), vmem_limit_bytes=limit * MIB)
    return pltpu.CompilerParams(collective_id=name_id, has_side_effects=True, vmem_limit_bytes=limit * MIB)


def greet(peers):
    barrier = pltpu.get_barrier_semaphore()
    for axis, index in peers:
        pl.semaphore_signal(barrier, inc=1, device_id={axis: index}, device_id_type=MESH)
    return lambda: pl.semaphore_wait(barrier, len(peers))


def remote(src, dst, send, recv, axis, index):
    return pltpu.make_async_remote_copy(src_ref=src, dst_ref=dst, send_sem=send, recv_sem=recv, device_id={axis: index}, device_id_type=MESH)


def silu(v):
    return v * (1.0 / (1.0 + jnp.exp(-v)))


def head_lanes(cols, tile_idx, head_dim):
    rows = cols.shape[0]
    per = LANES // head_dim
    lane = lax.broadcasted_iota(jnp.int32, (rows, LANES), 1)
    out = None
    for j in range(per):
        h = tile_idx * per + j
        nxt = jnp.broadcast_to(cols[:, h:h + 1], (rows, LANES))
        out = nxt if out is None else jnp.where(lane >= j * head_dim, nxt, out)
    return out


def expand_heads(row, head_dim):
    heads = row.shape[1]
    shape = (heads, heads * head_dim)
    eye = (lax.broadcasted_iota(jnp.int32, shape, 1) // head_dim == lax.broadcasted_iota(jnp.int32, shape, 0)).astype(F32)
    return jnp.dot(jnp.broadcast_to(row, (ROW8, heads)), eye, precision=HI, preferred_element_type=F32)[0:1]


def column(row):
    return jnp.broadcast_to(row, (LANES, row.shape[1])).T[:, 0:1]


def gather_kernel(chips, blocks, kb, nb, sub, nt, pace, x_ref, wzx_ref, wbc_ref, wdt_ref, wo_ref, seg_ref,
                  xf_ref, xp_ref, bp_ref, wz_ref, wp_ref, segf_ref, segt_ref, tx_ref, tb_ref,
                  wx, wsm, xg, ost, bst, blk, bblk, zst, wdt,
                  ra_sem, rd_sem, so_sem, sf_sem, sd_sem, xl_sem, xs_sem, in_sem, zo_sem, bb_sem, dt_sem, oo_sem, bo_sem,
                  wp_sem, sg_sem, sr_sem, st_sem, hx_sem, hb_sem):
    me = lax.axis_index('tp')
    blk_id = lax.axis_index('sp')
    chip, core = me // CORES, odd(me)
    partner = CORES * chip + flip(core)
    near = [lax.rem(chip + chips - 1, chips), lax.rem(chip + 1, chips)]
    far = lax.rem(chip + chips // 2, chips)
    ring = [CORES * c + core for c in near]
    sp_next = lax.rem(blk_id + 1, blocks)
    n_tp = CORES * chips
    rows = x_ref.shape[0]
    quarters = xl_sem.shape[1]
    qr = rows // quarters
    d_model, inner = wx.shape
    heads = wdt.shape[0]
    n_state = bblk.shape[3]
    nk = d_model // kb
    nblk = nk * (inner // nb)
    opp = 2 + quarters
    last = opp + quarters // 2 - 1
    ready = greet([('tp', lax.rem(me + d, n_tp)) for d in range(1, n_tp)] + [('sp', sp_next), ('sp', lax.rem(blk_id + blocks - 1, blocks))])

    def row_of(lv, b):
        side = odd(b)
        other = jnp.where(lv < 2, lv, b // 2)
        cc = jnp.where(other == 1, flip(core), core)
        ch = jnp.where(lv < 2, chip, jnp.where(lv >= opp, far, jnp.where(side == 0, near[0], near[1])))
        q = jnp.where(lv < 2, b, jnp.where(lv >= opp, side * (quarters // 2) + lv - opp, lv - 2))
        return (CORES * ch + cc) * rows + q * qr

    def full_rows(lv, b, size=qr):
        return xf_ref.at[rows_at(row_of(lv, b), size), :]

    def w_tile(i):
        return rows_at(lax.rem(i, nk) * kb, kb), rows_at((i // nk) * nb, nb)

    def blk_copy(i):
        kk, nn = w_tile(i)
        slot = lax.rem(i, blk.shape[0])
        return pltpu.make_async_copy(wzx_ref.at[kk, :, nn], blk.at[slot], in_sem.at[slot])

    def z_copy(i):
        kk, nn = w_tile(i)
        return pltpu.make_async_copy(zst.at[odd(i)], wz_ref.at[kk, nn], zo_sem.at[odd(i)])

    def bc_copy(i):
        return pltpu.make_async_copy(wbc_ref.at[rows_at(i * kb, kb)], bblk.at[odd(i)], bb_sem.at[odd(i)])

    own_load = pltpu.make_async_copy(x_ref, xg.at[0], xs_sem.at[0])
    dt_load = pltpu.make_async_copy(wdt_ref, wdt, dt_sem)
    own_load.start()
    dt_load.start()
    bc_copy(0).start()
    for i in range(blk.shape[0]):
        blk_copy(i).start()
    ready()

    def own_send(q, to):
        return remote(x_ref.at[rows_at(q * qr, qr), :], full_rows(0, q), so_sem.at[to, q], ra_sem.at[2 + q, flip(to)], 'tp', ring[to])

    own_pair = remote(x_ref, full_rows(0, 0, rows), sd_sem.at[1, 0], rd_sem.at[1, 0], 'tp', partner)

    def pair_send(lv, side):
        return remote(full_rows(lv, side), full_rows(lv, side), sd_sem.at[lv, side], rd_sem.at[lv, side], 'tp', partner)

    def forward(lv, to):
        side = flip(to)
        h = lax.rem(lv - 2, quarters // 2)
        dst_sem = ra_sem.at[opp + h, side]
        return remote(full_rows(lv, side), full_rows(lv, side), sf_sem.at[to, h], dst_sem, 'tp', ring[to])

    def arrival(lv, side):
        return remote(full_rows(lv, side), full_rows(lv, side), so_sem.at[0, 0], ra_sem.at[lv, side], 'tp', ring[0])

    def pair_arrival(lv, side):
        ref = full_rows(lv, 2 + side)
        return remote(ref, ref, sd_sem.at[1, 0], rd_sem.at[lv, side], 'tp', partner)

    pair_own_arrival = remote(full_rows(1, 0, rows), full_rows(1, 0, rows), sd_sem.at[1, 0], rd_sem.at[1, 0], 'tp', partner)

    def send_quarter(q):
        for to in PAIR:
            own_send(q, flip(to)).start()
    send_quarter(0)
    own_pair.start()

    def seg_cols(index):
        return segf_ref.at[:, rows_at(index * rows, rows)]

    def seg_send(d):
        return remote(seg_ref, seg_cols(me), sg_sem.at[d], sr_sem.at[d], 'tp', lax.rem(me + d, n_tp))

    def seg_arrival(d):
        return remote(seg_ref, seg_cols(lax.rem(me + n_tp - d, n_tp)), sg_sem.at[d], sr_sem.at[d], 'tp', lax.rem(me + d, n_tp))

    seg_own = pltpu.make_async_copy(seg_ref, seg_cols(me), sg_sem.at[0])
    seg_own.start()
    for d in range(1, n_tp):
        seg_send(d).start()
    w_swap = remote(wo_ref, wp_ref, wp_sem.at[0], wp_sem.at[1], 'tp', partner)
    w_swap.start()
    seg_halo = remote(segf_ref.at[:, pl.ds(n_tp * rows - LANES, LANES)], segt_ref, st_sem.at[0], st_sem.at[1], 'sp', sp_next)

    end_chip = chips - 1
    hrows = tx_ref.shape[0]
    halo_lv = jnp.where(chip == end_chip, flip(core), jnp.where(far == end_chip, last, opp - 1))
    halo_b = jnp.where(chip == end_chip, quarters - 1, jnp.where((far != end_chip) & (near[0] == end_chip), 0, 1) + CORES * flip(core))

    def halo_copies(slot):
        src = rows_at(halo_b * qr + qr - hrows, hrows)
        return [remote(ost.at[slot, src, :], tx_ref, hx_sem.at[0], hx_sem.at[1], 'sp', sp_next),
                remote(bst.at[slot, src, :], tb_ref, hb_sem.at[0], hb_sem.at[1], 'sp', sp_next)]

    dt_load.wait()

    def small_body(i, carry):
        bc_copy(i).wait()

        @pl.when(i + 1 < nk)
        def _():
            bc_copy(i + 1).start()

        def inner_body(s, carry2):
            part = jnp.swapaxes(bblk[odd(i), rows_at(s * sub, sub)], 0, 1)
            at = rows_at(i * kb + s * sub, sub)
            for g in PAIR:
                wsm[at, g * n_state:(g + 1) * n_state] = part[g]
            wd = jnp.concatenate([wdt[:, at].astype(F32), jnp.zeros((LANES - heads, sub), F32)], axis=0)
            wsm[at, 2 * n_state:] = wd.T.astype(BF16)
            return carry2
        return lax.fori_loop(0, kb // sub, inner_body, carry)
    lax.fori_loop(0, nk, small_body, 0)

    def relay(i, carry):
        slot = lax.rem(i, blk.shape[0])
        blk_copy(i).wait()

        @pl.when(i >= 2)
        def _():
            z_copy(i - 2).wait()
        kk = lax.rem(i, nk) * kb

        def inner_body(s, carry2):
            at = rows_at(s * sub, sub)
            part = jnp.swapaxes(blk[slot, at].astype(F32), 0, 1)
            zst[odd(i), at, :] = part[0].astype(BF16)
            wx[rows_at(kk + s * sub, sub), w_tile(i)[1]] = part[1].astype(BF16)
            return carry2
        lax.fori_loop(0, kb // sub, inner_body, 0)
        z_copy(i).start()
        for q in range(1, quarters - 1):
            pl.when(i == q * pace - 1)(functools.partial(send_quarter, q))

        @pl.when(i + blk.shape[0] < nblk)
        def _():
            blk_copy(i + blk.shape[0]).start()
        return carry
    lax.fori_loop(0, nblk, relay, 0)

    seg_own.wait()
    for d in range(1, n_tp):
        seg_arrival(d).wait_recv()
    seg_halo.start()
    own_load.wait()
    own_store = pltpu.make_async_copy(xg.at[0], full_rows(0, 0, rows), xs_sem.at[1])
    own_store.start()

    def load(lv, b):
        return pltpu.make_async_copy(full_rows(lv, b), xg.at[odd(lv), rows_at(b * qr, qr), :], xl_sem.at[odd(lv), b])

    def take(lv):
        @pl.when(lv >= 2)
        def _():
            for side in PAIR:
                arrival(lv, side).wait_recv()
                pair_send(lv, side).start()

    def fetch(lv):
        @pl.when(lv == 1)
        def _():
            pair_own_arrival.wait_recv()

        @pl.when(lv >= 2)
        def _():
            for side in PAIR:
                pair_arrival(lv, side).wait_recv()
        for b in range(quarters):
            load(lv, b).start()

    def out_copies(lv):
        slot = odd(lv)
        res = []
        for b in range(quarters):
            src, dst = rows_at(b * qr, qr), rows_at(row_of(lv, b), qr)
            res.append(pltpu.make_async_copy(ost.at[slot, src, :], xp_ref.at[dst, :], oo_sem.at[slot, b]))
            res.append(pltpu.make_async_copy(bst.at[slot, src, :], bp_ref.at[dst, :], bo_sem.at[slot, b]))
        return res

    early = opp - 1
    cut = 2 + quarters // 2

    def feed(lv):
        @pl.when(lv == 1)
        def _():
            send_quarter(quarters - 1)
        for h in range(quarters // 2):
            @pl.when(lv == 3 + 2 * h)
            def _(h=h):
                forward(2 + h, 1).start()
                forward(cut + h, 0).start()

    def round_body(lv, carry):
        slot = odd(lv)

        @pl.when(lv > 0)
        def _():
            for b in range(quarters):
                load(lv, b).wait()

        @pl.when(lv == 1)
        def _():
            own_store.wait()

        @pl.when(lv < early)
        def _():
            take(lv + 1)

        @pl.when(lv >= 2)
        def _():
            for cp in out_copies(lv - 2):
                cp.wait()

        def dots(n, carry2):
            @pl.when(n == inner // nt // 2)
            def _():
                feed(lv)

                @pl.when(lv < early)
                def _():
                    fetch(lv + 1)
            cols = rows_at(n * nt, nt)
            ost[slot, :, cols] = dot32(xg[slot], wx[:, cols]).astype(BF16)
            return carry2
        lax.fori_loop(0, inner // nt, dots, 0)
        bst[slot] = dot32(xg[slot], wsm[...]).astype(BF16)
        for cp in out_copies(lv):
            cp.start()

        @pl.when(lv == halo_lv + 1)
        def _():
            for cp in halo_copies(flip(slot)):
                cp.wait_send()

        @pl.when(lv == halo_lv)
        def _():
            for cp in halo_copies(slot):
                cp.start()

        @pl.when((lv >= early) & (lv < last))
        def _():
            take(lv + 1)
            fetch(lv + 1)
        return carry
    lax.fori_loop(0, last + 1, round_body, 0)

    @pl.when(halo_lv == last)
    def _():
        for cp in halo_copies(last % 2):
            cp.wait_send()
    for cp in halo_copies(0):
        cp.wait_recv()
    seg_halo.wait()
    for d in range(1, n_tp):
        seg_send(d).wait_send()
    w_swap.wait()
    for i in PAIR:
        for cp in out_copies(last - i):
            cp.wait()
        z_copy(nblk - 1 - i).wait()
    own_pair.wait_send()
    for to in PAIR:
        for q in range(quarters):
            own_send(q, to).wait_send()
        for h in range(quarters // 2):
            forward(2 + h, to).wait_send()
    for lv in range(2, last + 1):
        for side in PAIR:
            pair_send(lv, side).wait_send()


def gather_proj(x_loc, w_zx, w_bc, w_dt_t, w_out, seg, chips, blocks, kb=2048, nb=256, sub=256, nt=512, quarters=4, pace=12):
    rows, d_model = x_loc.shape
    inner, n_state, heads = w_zx.shape[2], w_bc.shape[2], w_dt_t.shape[0]
    n_tp = CORES * chips
    t = rows * n_tp
    small = CORES * n_state + LANES
    lv = CORES + quarters + quarters // 2
    halo = 16
    two = sems(2)
    return pl.pallas_call(
        functools.partial(gather_kernel, chips, blocks, kb, nb, sub, nt, pace),
        in_specs=[ANY] * 6,
        out_specs=[ANY] * 9,
        out_shape=[out_of(BF16, t, d_model), out_of(BF16, t, inner), out_of(BF16, t, small), out_of(BF16, d_model, inner), out_of(BF16, *w_out.shape),
                   out_of(jnp.int32, 1, t), out_of(jnp.int32, 1, LANES), out_of(BF16, halo, inner), out_of(BF16, halo, small)],
        scratch_shapes=[scratch(BF16, d_model, inner), scratch(BF16, d_model, small), scratch(BF16, 2, rows, d_model),
                        scratch(BF16, 2, rows, inner), scratch(BF16, 2, rows, small), scratch(BF16, 3, kb, CORES, nb),
                        scratch(BF16, 2, kb, CORES, n_state), scratch(BF16, 2, kb, nb), scratch(BF16, heads, d_model),
                        sems(lv, 2), sems(lv, 2), sems(2, quarters), sems(2, quarters), sems(lv, 2), sems(2, quarters), two, sems(3), two, two, DMA,
                        sems(2, quarters), sems(2, quarters), two, sems(n_tp), sems(n_tp), two, two, two],
        compiler_params=params(63, 0),
        cost_estimate=pl.CostEstimate(flops=t * inner * d_model, bytes_accessed=t * inner, transcendentals=0),
        name='gather_proj',
    )(x_loc, w_zx, w_bc, w_dt_t, w_out, seg)


def phase_a_kernel(q, x_ref, small_ref, seg_ref, segt_ref, tailx_ref, tailb_ref, cx_ref, cbc_ref, bx_ref, bbc_ref, alog_ref, dtb_ref,
                   xact_ref, bcact_ref, cum_ref, cl_ref, segf_ref, segp_ref, sloc_ref, pd_ref, send_ref, dec_ref,
                   pad, xw, state, segtail, base, cw):
    inner = x_ref.shape[1]
    gw = bcact_ref.shape[1]
    n_state = gw // 2
    heads = alog_ref.shape[1]
    head_dim = inner // heads
    taps = cx_ref.shape[0]

    @pl.when(pl.program_id(0) == 0)
    def _():
        first = lax.axis_index('sp') == 0
        base[...] = jnp.broadcast_to(jnp.where(first, seg_ref[:, 0:1], segt_ref[:, LANES - 1:]), base.shape)
        segtail[...] = jnp.where(first, FAR, (segt_ref[...] - base[...]).astype(F32))
        pad[0:ROW8, 0:inner] = tailx_ref[...].astype(F32)[ROW8:]
        pad[0:ROW8, inner:] = tailb_ref[:, 0:gw].astype(F32)[ROW8:]
        cw[0:taps, 0:inner] = cx_ref[...].astype(F32)
        cw[taps:taps + 1, 0:inner] = bx_ref[...].astype(F32)
        for g in PAIR:
            cols = slice(inner + g * n_state, inner + (g + 1) * n_state)
            cw[0:taps, cols] = cbc_ref[:, g, :].astype(F32)
            cw[taps:taps + 1, cols] = bbc_ref[g:g + 1, :].astype(F32)
        state[...] = jnp.zeros_like(state)
        dec_ref[...] = jnp.ones_like(dec_ref)

    @pl.when(pl.program_id(0) > 0)
    def _():
        pad[0:ROW8, :] = pad[q:q + ROW8, :]

    pad[ROW8:, 0:inner] = x_ref[...].astype(F32)
    pad[ROW8:, inner:] = small_ref[:, 0:gw].astype(F32)
    seg_row = (seg_ref[...] - base[:, 0:1]).astype(F32)
    prev_row = segtail[...]
    segf_ref[...] = seg_row
    segp_ref[0] = prev_row
    segtail[...] = seg_row[:, q - LANES:]
    ext = jnp.concatenate([prev_row, seg_row], axis=1)
    seg_last, seg_prev = seg_row[:, q - 1:], prev_row[:, LANES - 1:]
    keeps = []
    for j in range(1, taps):
        keep_row = jnp.where(ext[:, LANES - j:LANES - j + q] == seg_row, 1.0, 0.0)
        keeps.append(jnp.broadcast_to(keep_row, (LANES, q)).T)
    for i in range((inner + gw) // LANES):
        cols = slice(i * LANES, (i + 1) * LANES)
        acc = cw[taps:taps + 1, cols] + pad[ROW8:, cols] * cw[taps - 1:taps, cols]
        for j in range(1, taps):
            at = taps - 1 - j
            acc = acc + pad[ROW8 - j:q + ROW8 - j, cols] * cw[at:at + 1, cols] * keeps[j - 1]
        act = silu(acc).astype(BF16)
        if i * LANES < inner:
            xact_ref[:, cols] = act
        else:
            bcact_ref[:, i * LANES - inner:(i + 1) * LANES - inner] = act
    raw = small_ref[:, gw:].astype(F32).T[0:heads] + column(dtb_ref[...])
    dt = jnp.maximum(raw, 0.0) + jnp.log1p(jnp.exp(-jnp.abs(raw)))
    log_a = dt * column(jnp.exp(alog_ref[...]) * -LOG2E)
    tri = (lax.broadcasted_iota(jnp.int32, (q, q), 0) <= lax.broadcasted_iota(jnp.int32, (q, q), 1)).astype(F32)
    cum = jnp.dot(log_a, tri, precision=HI, preferred_element_type=F32)
    cum_ref[...] = cum
    cl_ref[...] = cum - jnp.log(dt) * LOG2E
    cum_last = cum[:, q - 1:]
    end_cols = (jnp.where(seg_row == seg_last, jnp.exp2(cum_last - cum), 0.0) * dt).T
    carry = jnp.where(seg_last == seg_prev, jnp.exp2(cum_last), 0.0)
    carry_lane = expand_heads(jnp.broadcast_to(carry, (heads, LANES)).T[0:1], head_dim)
    for i in range(inner // LANES):
        cols = slice(i * LANES, (i + 1) * LANES)
        xw[:, cols] = (xact_ref[:, cols].astype(F32) * head_lanes(end_cols, i, head_dim)).astype(BF16)
    sloc_ref[0] = state[...]
    pd_ref[0] = dec_ref[...]
    new_state = carry_lane * state[...] + dot32(bcact_ref[:, 0:n_state].T, xw[...])
    state[...] = new_state
    send_ref[...] = new_state
    dec_ref[...] = dec_ref[...] * carry_lane


def phase_a(x_pre, small, seg, seg_tail, tail_x, tail_b, conv_x, conv_bc, bias_x, bias_bc, a_log, dt_bias, q):
    t, inner = x_pre.shape
    n_state = conv_bc.shape[2]
    gw = CORES * n_state
    heads = a_log.shape[1]
    nt = t // q

    def full(shape):
        return pl.BlockSpec(shape, lambda c: (0,) * len(shape))

    def by_row(width):
        return pl.BlockSpec((q, width), lambda c: (c, 0))

    def by_col(height):
        return pl.BlockSpec((height, q), lambda c: (0, c))

    def by_chunk(a, b):
        return pl.BlockSpec((1, a, b), lambda c: (c, 0, 0))

    rest = (seg_tail, tail_x, tail_b, conv_x, conv_bc, bias_x, bias_bc, a_log, dt_bias)
    return pl.pallas_call(
        functools.partial(phase_a_kernel, q),
        grid=(nt,),
        in_specs=[by_row(inner), by_row(small.shape[1]), by_col(1)] + [full(v.shape) for v in rest],
        out_specs=[by_row(inner), by_row(gw), by_col(heads), by_col(heads), by_col(1), by_chunk(1, LANES), by_chunk(n_state, inner), by_chunk(1, inner),
                   full((n_state, inner)), full((1, inner))],
        out_shape=[out_of(BF16, t, inner), out_of(BF16, t, gw), out_of(F32, heads, t), out_of(F32, heads, t), out_of(F32, 1, t), out_of(F32, nt, 1, LANES),
                   out_of(F32, nt, n_state, inner), out_of(F32, nt, 1, inner), out_of(F32, n_state, inner), out_of(F32, 1, inner)],
        scratch_shapes=[scratch(F32, q + ROW8, inner + gw), scratch(BF16, q, inner), scratch(F32, n_state, inner), scratch(F32, 1, LANES),
                        scratch(jnp.int32, 1, LANES), scratch(F32, ROW8, inner + gw)],
        compiler_params=params(56),
        cost_estimate=pl.CostEstimate(flops=t * inner * gw, bytes_accessed=t * inner, transcendentals=0),
        name='phase_a',
    )(x_pre, small, seg, *rest)


def chain_kernel(chips, blocks, pieces, hop, nt, xf_ref, wz_ref, send_ref, dec_ref, z_ref, sin_ref,
                 xg, wzb, zst, sbuf, rbuf, x_sem, w_sem, z_sem, s_sem, r_sem):
    chip = lax.axis_index('tp') // CORES
    blk_id = lax.axis_index('sp')
    sp_next = lax.rem(blk_id + 1, blocks)
    ready = greet([('sp', sp_next), ('sp', lax.rem(blk_id + blocks - 1, blocks))])
    n_state, inner = send_ref.shape
    tm = xg.shape[1]
    nn = inner // nt
    tiles = CORES * nn
    pw = inner // pieces

    def tok(g):
        return rows_at(lax.rem(chip + jnp.where(g == 0, chips - 1, 1), chips) * tm, tm)

    def col(i):
        return rows_at(lax.rem(i, nn) * nt, nt)

    def x_copy(g):
        return pltpu.make_async_copy(xf_ref.at[tok(g), :], xg.at[g], x_sem.at[g])

    def w_copy(i):
        return pltpu.make_async_copy(wz_ref.at[:, col(i)], wzb.at[odd(i)], w_sem.at[odd(i)])

    def z_copy(i):
        return pltpu.make_async_copy(zst.at[odd(i)], z_ref.at[tok(i // nn), col(i)], z_sem.at[odd(i)])

    def hop_copy(p):
        return remote(sbuf.at[p], rbuf.at[p], s_sem.at[p], r_sem.at[p], 'sp', sp_next)

    for g in PAIR:
        x_copy(g).start()
    w_copy(0).start()
    ready()

    def body(i, carry):
        p = i - hop * blk_id

        @pl.when((p >= 0) & (p < pieces))
        def _():
            cols = rows_at(p * pw, pw)

            @pl.when(blk_id == 0)
            def _():
                sbuf[p] = send_ref[:, cols]
                sin_ref[:, cols] = jnp.zeros((n_state, pw), F32)

            @pl.when(blk_id > 0)
            def _():
                hop_copy(p).wait_recv()
                prev = rbuf[p]
                sin_ref[:, cols] = prev
                sbuf[p] = dec_ref[:, cols] * prev + send_ref[:, cols]

            @pl.when(blk_id < blocks - 1)
            def _():
                hop_copy(p).start()

        @pl.when(i < tiles)
        def _():
            g = i // nn

            @pl.when(lax.rem(i, nn) == 0)
            def _():
                x_copy(g).wait()
            w_copy(i).wait()

            @pl.when(i + 1 < tiles)
            def _():
                w_copy(i + 1).start()

            @pl.when(i >= 2)
            def _():
                z_copy(i - 2).wait()
            zst[odd(i)] = dot32(xg[g], wzb[odd(i)]).astype(BF16)
            z_copy(i).start()
        return carry

    lax.fori_loop(0, max(tiles, hop * (blocks - 1) + pieces), body, 0)
    for i in PAIR:
        z_copy(tiles - 1 - i).wait()

    @pl.when(blk_id < blocks - 1)
    def _():
        for p in range(pieces):
            hop_copy(p).wait_send()


def z_chain(x_full, w_z, s_end, dec, chips, blocks, pieces=4, hop=2, nt=512):
    t, d_model = x_full.shape
    n_state, inner = s_end.shape
    tm = t // chips
    piece = scratch(F32, pieces, n_state, inner // pieces)
    two = sems(2)
    return pl.pallas_call(
        functools.partial(chain_kernel, chips, blocks, pieces, hop, nt),
        in_specs=[ANY, ANY, VMEM, VMEM],
        out_specs=[ANY, VMEM],
        out_shape=[out_of(BF16, t, inner), out_of(F32, n_state, inner)],
        scratch_shapes=[scratch(BF16, 2, tm, d_model), scratch(BF16, 2, d_model, nt), scratch(BF16, 2, tm, nt), piece, piece,
                        two, two, two, sems(pieces), sems(pieces)],
        compiler_params=params(60, 2),
        cost_estimate=pl.CostEstimate(flops=t * inner * d_model, bytes_accessed=t * inner, transcendentals=0),
        name='z_chain',
    )(x_full, w_z, s_end, dec)


def out_kernel(chips, nb, wc, slots, zt, xact_ref, bc_ref, cum_ref, cl_ref, seg_ref, segp_ref, sloc_ref, pd_ref, sin_ref, z_ref, xf_ref, wz_ref,
               dskip_ref, nw_ref, wo_ref, wp_ref, x_ref, o_ref, recv_ref,
               va_own, va_par, wbuf, send, rbuf, xo, xg, wzb, zb, xa, bca, sl, sbf, yoff, gated, dlane,
               vs_sem, vr_sem, w_sem, s_sem, r_sem, l_sem, x_sem, o_sem, c_sem, z_sem):
    me = lax.axis_index('tp')
    chip, core = me // CORES, odd(me)
    partner = CORES * chip + flip(core)
    chip_at = lambda d: lax.rem(chip + d, chips)
    ring = [CORES * chip_at(chips - 1) + core, CORES * chip_at(1) + core]
    q = va_own.shape[1]
    inner = xa.shape[1]
    heads = cum_ref.shape[0]
    head_dim = inner // heads
    per = LANES // head_dim
    n_state = sl.shape[0]
    half_cols = nb * wc
    steps = chips * nb * 2
    hq = q // 2
    ready = greet([('tp', partner)] + [('tp', r) for r in ring])

    def cols_of(u):
        return rows_at(odd(u) * half_cols + lax.rem(u // 2, nb) * wc, wc)

    def w_copies(u):
        slot = odd(u)
        return [pltpu.make_async_copy(ref.at[:, cols_of(u)], wbuf.at[slot, i], w_sem.at[slot, i]) for i, ref in enumerate((wo_ref, wp_ref))]

    for cp in w_copies(0):
        cp.start()
    x_copy = pltpu.make_async_copy(x_ref, xo, x_sem)
    x_copy.start()
    dlane[...] = expand_heads(dskip_ref[...], head_dim)
    ready()

    def swap(n, j):
        return remote(va_own.at[chips + odd(n)], va_par.at[j], vs_sem.at[n], vr_sem.at[n], 'tp', partner)

    def mix(c, zrow, tgt):
        at = rows_at(c * q, q)
        copies = [pltpu.make_async_copy(xact_ref.at[at, :], xa, c_sem.at[0]), pltpu.make_async_copy(bc_ref.at[at, :], bca, c_sem.at[1]),
                  pltpu.make_async_copy(sloc_ref.at[c], sl, c_sem.at[2])]
        for cp in copies:
            cp.start()
        seg_row = seg_ref[:, at]
        seg_prev = segp_ref[c][:, LANES - 1:]
        seg_rows = jnp.broadcast_to(seg_row, (q, q))
        causal = lax.broadcasted_iota(jnp.int32, (q, q), 0) >= lax.broadcasted_iota(jnp.int32, (q, q), 1)
        bias = jnp.where(causal & (seg_rows == seg_rows.T), 0.0, NEG)
        cum = cum_ref[:, at]
        cl = cl_ref[:, at]
        cum_cols = cum.T
        in_cols = jnp.where(seg_row == seg_prev, jnp.exp2(cum), 0.0).T
        for cp in copies:
            cp.wait()
        sbf[...] = (sl[...] + pd_ref[c] * sin_ref[...]).astype(BF16)
        c_act = bca[:, n_state:]
        scores = lax.dot_general(c_act, bca[:, 0:n_state], (((1,), (1,)), ((), ())), preferred_element_type=F32)
        yoff[...] = dot32(c_act, sbf[...])
        lane = lax.broadcasted_iota(jnp.int32, (q, LANES), 1) // head_dim
        sq = jnp.zeros((q, LANES), F32)
        for i in range(inner // LANES):
            cols = slice(i * LANES, (i + 1) * LANES)
            x_f = xa[:, cols].astype(F32)
            tops, bots = [], []
            for j in range(per):
                h = i * per + j
                x_h = jnp.where(lane == j, x_f, 0.0).astype(BF16)
                ccol, crow = cum_cols[:, h:h + 1], cl[h:h + 1, :]
                m_top = jnp.exp2(ccol[0:hq] + bias[0:hq, 0:hq] - crow[:, 0:hq]) * scores[0:hq, 0:hq]
                m_bot = jnp.exp2(ccol[hq:] + bias[hq:] - crow) * scores[hq:]
                tops.append(dot32(m_top.astype(BF16), x_h[0:hq]))
                bots.append(dot32(m_bot.astype(BF16), x_h))
            y = jnp.concatenate([sum(tops), sum(bots)], axis=0)
            y = y + yoff[:, cols] * head_lanes(in_cols, i, head_dim) + dlane[:, cols] * x_f
            v = y * silu(zb[zrow, :, cols].astype(F32))
            gated[:, cols] = v
            sq = sq + v * v
        inv = lax.rsqrt(jnp.sum(sq, axis=1, keepdims=True) * (1.0 / inner) + NORM_EPS)
        inv = jnp.broadcast_to(inv, (q, LANES))
        for i in range(inner // LANES):
            cols = slice(i * LANES, (i + 1) * LANES)
            va_own[tgt, :, cols] = (gated[:, cols] * inv * nw_ref[:, cols].astype(F32)).astype(BF16)

    def prep(n):
        j = chip_at(jnp.where(n == 0, chips - 1, jnp.where(n == 3, 0, n)))
        tok = rows_at(j * (CORES * q), CORES * q)

        @pl.when(n < 2)
        def _():
            for p in PAIR:
                pltpu.make_async_copy(z_ref.at[rows_at((CORES * j + p) * q, q), :], zb.at[p], c_sem.at[p]).start()
            for p in PAIR:
                pltpu.make_async_copy(z_ref.at[rows_at((CORES * j + p) * q, q), :], zb.at[p], c_sem.at[p]).wait()

        @pl.when(n >= 2)
        def _():
            def wz_copy(m):
                return pltpu.make_async_copy(wz_ref.at[:, rows_at(m * zt, zt)], wzb.at[odd(m)], z_sem.at[odd(m)])
            rows_copy = pltpu.make_async_copy(xf_ref.at[tok, :], xg, c_sem.at[0])
            rows_copy.start()
            wz_copy(0).start()
            rows_copy.wait()

            def z_body(m, carry):
                wz_copy(m).wait()

                @pl.when(m + 1 < inner // zt)
                def _():
                    wz_copy(m + 1).start()
                res = dot32(xg[...], wzb[odd(m)]).astype(BF16)
                for p in PAIR:
                    zb[p, :, rows_at(m * zt, zt)] = res[p * q:(p + 1) * q]
                return carry
            lax.fori_loop(0, inner // zt, z_body, 0)

            swap(n - 2, j).wait_send()

        def chunk(i, carry):
            par = jnp.where(i == 0, flip(core), core)
            mix(CORES * j + par, par, jnp.where(i == 0, chips + odd(n), j))

            @pl.when(i == 0)
            def _():
                swap(n, j).start()
            return carry
        lax.fori_loop(0, CORES, chunk, 0)
        swap(n, j).wait_recv()

    def ring_copy(d, unit):
        slot = lax.rem(unit, slots)
        return remote(send.at[d, slot], recv_ref.at[d, unit], s_sem.at[d, slot], r_sem.at[d, unit], 'tp', jnp.where(d == 0, ring[1], ring[0]))

    def fetch(d, unit):
        ring_copy(d, unit).wait_recv()
        cp = pltpu.make_async_copy(recv_ref.at[d, unit], rbuf, l_sem)
        cp.start()
        cp.wait()

    def o_copy(d, b):
        cols = rows_at(d * half_cols + b * wc, wc)
        return pltpu.make_async_copy(xo.at[:, cols], o_ref.at[:, cols], o_sem.at[d, b])

    def body(u, carry):
        d = odd(u)
        k = u // (2 * nb)
        b = lax.rem(u // 2, nb)
        unit = k * nb + b

        @pl.when((u < 2) | ((b == 0) & (d == 0) & (k < chips - 1)))
        def _():
            prep(jnp.where(u < 2, u, k + 1))
        dest = chip_at(jnp.where(d == 0, 2 * chips - 1 - k, 1 + k))
        for cp in w_copies(u):
            cp.wait()

        @pl.when(u + 1 < steps)
        def _():
            for cp in w_copies(u + 1):
                cp.start()
        part = dot32(va_own[dest], wbuf[odd(u), 0]) + dot32(va_par[dest], wbuf[odd(u), 1])

        @pl.when(k < chips - 1)
        def _():
            slot = lax.rem(unit, slots)

            @pl.when(unit >= slots)
            def _():
                ring_copy(d, unit - slots).wait_send()

            @pl.when(k == 0)
            def _():
                send[d, slot] = part

            @pl.when(k > 0)
            def _():
                fetch(d, unit - nb)
                send[d, slot] = part + rbuf[...]
            ring_copy(d, unit).start()

        @pl.when(k == chips - 1)
        def _():
            @pl.when((b == 0) & (d == 0))
            def _():
                x_copy.wait()
            fetch(d, unit - nb)
            cols = cols_of(u)
            xo[:, cols] = (xo[:, cols].astype(F32) + (part + rbuf[...])).astype(BF16)
            o_copy(d, b).start()
        return carry

    lax.fori_loop(0, steps, body, 0)

    def drain(i, carry):
        o_copy(odd(i), i // 2).wait()
        return carry

    def drain_send(i, carry):
        ring_copy(odd(i), (chips - 1) * nb - slots + i // 2).wait_send()
        return carry
    lax.fori_loop(0, 2 * slots, drain_send, 0)
    for n in PAIR:
        swap(2 + n, chip).wait_send()
    lax.fori_loop(0, 2 * nb, drain, 0)


def out_proj_scatter(x_act, bc_act, cum, cl, seg_row, seg_prev, sloc, pd, s_in, z_arr, x_full, w_z, d_skip, norm_w, w_own, w_par, x_loc, chips, wc=512, slots=4, zt=256):
    t, inner = x_act.shape
    rows, d_model = x_loc.shape
    gw = bc_act.shape[1]
    n_state = s_in.shape[0]
    nb = d_model // 2 // wc
    units = (chips - 1) * nb
    return pl.pallas_call(
        functools.partial(out_kernel, chips, nb, wc, slots, zt),
        in_specs=[ANY, ANY, VMEM, VMEM, VMEM, VMEM, ANY, VMEM, VMEM, ANY, ANY, ANY, VMEM, VMEM, ANY, ANY, ANY],
        out_specs=[ANY, ANY],
        out_shape=[out_of(BF16, rows, d_model), out_of(F32, 2, units, rows, wc)],
        scratch_shapes=[scratch(BF16, chips + 2, rows, inner), scratch(BF16, chips, rows, inner), scratch(BF16, 2, 2, inner, wc), scratch(F32, 2, slots, rows, wc),
                        scratch(F32, rows, wc), scratch(BF16, rows, d_model), scratch(BF16, CORES * rows, d_model), scratch(BF16, 2, d_model, zt),
                        scratch(BF16, CORES, rows, inner), scratch(BF16, rows, inner), scratch(BF16, rows, gw), scratch(F32, n_state, inner),
                        scratch(BF16, n_state, inner), scratch(F32, rows, inner), scratch(F32, rows, inner), scratch(F32, 1, inner),
                        sems(chips), sems(chips), sems(2, 2), sems(2, slots), sems(2, units), DMA, DMA, sems(2, nb), sems(3), sems(2)],
        compiler_params=params(63, 1),
        cost_estimate=pl.CostEstimate(flops=2 * t * inner * d_model, bytes_accessed=t * d_model, transcendentals=0),
        name='out_proj_scatter',
    )(x_act, bc_act, cum, cl, seg_row, seg_prev, sloc, pd, s_in, z_arr, x_full, w_z, d_skip, norm_w, w_own, w_par, x_loc)[0]


def layer(x_loc, seg_loc, w_zx, w_bc, w_dt, conv_x, conv_bc, bias_x, bias_bc, a_log, dt_bias, d_skip, norm_w, w_out, chips, blocks):
    rows = x_loc.shape[0]
    x_full, x_pre, small, w_z, w_par, seg, seg_tail, tail_x, tail_b = gather_proj(x_loc, w_zx, w_bc, w_dt.T, w_out, seg_loc[None], chips, blocks)
    x_act, bc_act, cum, cl, seg_row, seg_prev, sloc, pd, s_end, dec = phase_a(
        x_pre, small, seg, seg_tail, tail_x, tail_b, conv_x, conv_bc, bias_x[None], bias_bc, a_log[None], dt_bias[None], rows)
    z_arr, s_in = z_chain(x_full, w_z, s_end, dec, chips, blocks)
    return out_proj_scatter(x_act, bc_act, cum, cl, seg_row, seg_prev, sloc, pd, s_in, z_arr, x_full, w_z, d_skip[None], norm_w[None], w_out, w_par, x_loc, chips)


def solution(mesh):
    tokens = ('dp', 'sp', 'tp')
    heads = P('tp')
    cols = P(None, 'tp')
    deep = P(None, None, 'tp')
    specs = (P(tokens, None), P(tokens), deep, deep, cols, cols, deep, heads, cols, heads, heads, heads, heads, P('tp', None))
    body = functools.partial(layer, chips=mesh.shape['tp'] // CORES, blocks=mesh.shape['sp'])
    return jax.shard_map(body, mesh=mesh, in_specs=specs, out_specs=specs[0], check_vma=False)
```

time: 1570 us -> 561 us (0.36)
  Pallas kernels: 0 us -> 552 us
  local copies, waits for them, and re-layouts: 532 us -> 7.21 us
  waiting for transfers between devices: 492 us -> 0 us
  matrix products: 357 us -> 0 us
  other arithmetic: 99.5 us -> 0 us
  starting transfers between devices: 28.1 us -> 0 us
  blocking collectives: 18.9 us -> 0 us
    pallas_call x0 -> x4, Pallas kernels: none -> 552 us  [the longest x1 307 us: out_proj_scatter(): pl.pallas_call(functools.partial(out_kernel, chips, nb, wc, slots, zt), i...]
    dynamic_update_slice x16 -> x0, local copies, waits for them, and re-layouts: 396 us -> none  [block_ssd(): end_state, y_tiles = lax.scan(body, init_state, tiles_in)]
    dot_general x37 -> x0, matrix products: 357 us -> none  [the longest x1 154 us: local_layer(): jnp.einsum('ld,dkc->lkc', x_blk, w_zx, preferred_element_type=jnp.float32)]
    reduce_scatter x1 -> x0, waiting for transfers between devices: 328 us -> none  [body(): out_loc = lax.psum_scatter(out_part, 'tp', scatter_dimension=0, tiled=True)]
    all_gather x1 -> x0, waiting for transfers between devices: 127 us -> none  [body(): x_blk = lax.all_gather(x_loc, 'tp', axis=0, tiled=True)]
    convert_element_type x7 -> x0, other arithmetic: 41.1 us -> none  [the longest x2 29.6 us: causal_conv(): return jax.nn.silu(conv_acc).astype(jnp.bfloat16)]
    ppermute x8 -> x0, waiting for transfers between devices: 36.7 us -> none  [the longest x1 18 us: chain_state(): prev_decay = lax.ppermute(decay_in, seq_axis, hop_perm)]
    reshape x12 -> x0, local copies, waits for them, and re-layouts: 36.2 us -> none  [the longest x1 18.1 us: block_ssd(): return (end_state, y_tiles.reshape(row_count, groups, per_group, head_dim))]
  transfers between devices with their start and end apart: 10 -> 0, of which waited for: 5 -> 0; matrix products, arithmetic and copies ran while one was open for 15% -> 0% of each run, Pallas kernels for 0% -> 0%
where the time goes in v2:
time: 561 us; the launch traced here: 559 us
  Pallas kernels  552 us (98%)
  local copies, waits for them, and re-layouts  7.21 us (1%)
    pallas_call x1, Pallas kernels, out_proj_scatter(): pl.pallas_call(functools.partial(out_kernel, chips, nb, wc, slots, zt), i...  307 us
    pallas_call x1, Pallas kernels, gather_proj(): pl.pallas_call(functools.partial(gather_kernel, chips, blocks, kb, nb, su...  164 us
    pallas_call x1, Pallas kernels, z_chain(): pl.pallas_call(functools.partial(chain_kernel, chips, blocks, pieces, hop...  47.5 us
    pallas_call x1, Pallas kernels, phase_a(): pl.pallas_call(functools.partial(phase_a_kernel, q), grid=(nt,), in_specs...  33.4 us

profile of v2, /device:TPU:97, one launch (start us, length us, event | category | flops | bytes accessed | tf_op | source)
XLA Modules:
  0.0 559.3 jit_solution(5163989623348910594)
XLA Ops:
  0.0 1.3 broadcast_in_dim.19.bx_ref
  1.3 1.3 broadcast_in_dim.23.nw_ref
  2.6 164.3 %gather_proj.1 = (bf16[2048,8192]{1,0:T(8,128)(2,1)}, bf16[2048,2048]{1,0:T(8,128)(2,1)}, bf16[2048,384]{1,0:T(8,128)(2,1)}, bf16[8192,2048]{1,0:T(8,128)(2,1)},...) custom-call(bf16[256,8192]{1,0:T(8,128)(2,1)} %x_ref.3, ...), custom_call_target="tpu_custom_call" | custom-call | flops 34359738368 | bytes 4194304 | tf_op jit(solution)/shard_map/gather_proj/pallas_call | solution.py:402
  166.9 33.4 %phase_a.1 = (bf16[2048,2048]{1,0:T(8,128)(2,1)}, bf16[2048,256]{1,0:T(8,128)(2,1)}, f32[32,2048]{1,0:T(8,128)}, f32[32,2048]{1,0:T(8,128)}, f32[1,2048]{1,0:T(1...) custom-call(bf16[2048,2048]{1,0:T(8,128)(2,1)} %get-tuple-element.27, ...), custom_call_target="tpu_custom_call" | custom-call | flops 1073741824 | bytes 4194304 | tf_op jit(solution)/shard_map/phase_a/pallas_call | solution.py:515
  200.3 47.5 %z_chain.1 = (bf16[2048,2048]{1,0:T(8,128)(2,1)}, f32[128,2048]{1,0:T(8,128)}) custom-call(bf16[2048,8192]{1,0:T(8,128)(2,1)} %get-tuple-element.41.xf_ref, bf16[8192,2048]{1,0:T(8,128)(2,1)} %get-tuple-element.42.wz_ref, f32[128,2048]{1,0:T(8,128)} %get-tuple-element.43.send_ref, f32[1,2048]{1,0:T(1,128)} %get-tuple-element.44.dec_ref), custom_call_target="tpu_custom_call" | custom-call | flops 34359738368 | bytes 4194304 | tf_op jit(solution)/shard_map/z_chain/pallas_call | solution.py:625
  247.8 306.8 %out_proj_scatter.1 = (bf16[256,8192]{1,0:T(8,128)(2,1)}, f32[2,24,256,512]{3,2,1,0:T(8,128)}) custom-call(bf16[2048,2048]{1,0:T(8,128)(2,1)} %get-tuple-element.33.xact_ref, bf16[2048,256]{1,0:T(8,128)(2,1)} %get-tuple-element.34.bc_ref, f32[32,2048]{1,0:T(8,128)} %get-tuple-element.35.cum_ref, f32[32,2048]{1,0:T(8,128)} %get-tuple-element.36.cl_ref, ...), custom_call_target="tpu_custom_call" | custom-call | flops 68719476736 | bytes 16777216 | tf_op jit(solution)/shard_map/out_proj_scatter/pallas_call | solution.py:850
  554.6 4.6 copy.16

commit v3 on v2

--- a/solution.py
+++ b/solution.py
@@ -70,7 +70,8 @@
 
 
 def silu(v):
-    return v * (1.0 / (1.0 + jnp.exp(-v)))
+    h = v * 0.5
+    return h + h * jnp.tanh(h)
 
 
 def head_lanes(cols, tile_idx, head_dim):
@@ -418,7 +419,7 @@
 
 def phase_a_kernel(q, x_ref, small_ref, seg_ref, segt_ref, tailx_ref, tailb_ref, cx_ref, cbc_ref, bx_ref, bbc_ref, alog_ref, dtb_ref,
                    xact_ref, bcact_ref, cum_ref, cl_ref, segf_ref, segp_ref, sloc_ref, pd_ref, send_ref, dec_ref,
-                   pad, xw, state, segtail, base, cw):
+                   pad, xw, segtail, base, cw):
     inner = x_ref.shape[1]
     gw = bcact_ref.shape[1]
     n_state = gw // 2
@@ -434,12 +435,13 @@
         pad[0:ROW8, 0:inner] = tailx_ref[...].astype(F32)[ROW8:]
         pad[0:ROW8, inner:] = tailb_ref[:, 0:gw].astype(F32)[ROW8:]
         cw[0:taps, 0:inner] = cx_ref[...].astype(F32)
-        cw[taps:taps + 1, 0:inner] = bx_ref[...].astype(F32)
+        for i in range(inner // LANES):
+            cw[taps:taps + 1, i * LANES:(i + 1) * LANES] = bx_ref[i:i + 1, :].astype(F32)
         for g in PAIR:
             cols = slice(inner + g * n_state, inner + (g + 1) * n_state)
             cw[0:taps, cols] = cbc_ref[:, g, :].astype(F32)
             cw[taps:taps + 1, cols] = bbc_ref[g:g + 1, :].astype(F32)
-        state[...] = jnp.zeros_like(state)
+        send_ref[...] = jnp.zeros_like(send_ref)
         dec_ref[...] = jnp.ones_like(dec_ref)
 
     @pl.when(pl.program_id(0) > 0)
@@ -459,17 +461,6 @@
     for j in range(1, taps):
         keep_row = jnp.where(ext[:, LANES - j:LANES - j + q] == seg_row, 1.0, 0.0)
         keeps.append(jnp.broadcast_to(keep_row, (LANES, q)).T)
-    for i in range((inner + gw) // LANES):
-        cols = slice(i * LANES, (i + 1) * LANES)
-        acc = cw[taps:taps + 1, cols] + pad[ROW8:, cols] * cw[taps - 1:taps, cols]
-        for j in range(1, taps):
-            at = taps - 1 - j
-            acc = acc + pad[ROW8 - j:q + ROW8 - j, cols] * cw[at:at + 1, cols] * keeps[j - 1]
-        act = silu(acc).astype(BF16)
-        if i * LANES < inner:
-            xact_ref[:, cols] = act
-        else:
-            bcact_ref[:, i * LANES - inner:(i + 1) * LANES - inner] = act
     raw = small_ref[:, gw:].astype(F32).T[0:heads] + column(dtb_ref[...])
     dt = jnp.maximum(raw, 0.0) + jnp.log1p(jnp.exp(-jnp.abs(raw)))
     log_a = dt * column(jnp.exp(alog_ref[...]) * -LOG2E)
@@ -481,14 +472,22 @@
     end_cols = (jnp.where(seg_row == seg_last, jnp.exp2(cum_last - cum), 0.0) * dt).T
     carry = jnp.where(seg_last == seg_prev, jnp.exp2(cum_last), 0.0)
     carry_lane = expand_heads(jnp.broadcast_to(carry, (heads, LANES)).T[0:1], head_dim)
-    for i in range(inner // LANES):
+    for i in range((inner + gw) // LANES):
         cols = slice(i * LANES, (i + 1) * LANES)
-        xw[:, cols] = (xact_ref[:, cols].astype(F32) * head_lanes(end_cols, i, head_dim)).astype(BF16)
-    sloc_ref[0] = state[...]
+        src = pad[:, cols]
+        acc = cw[taps:taps + 1, cols] + src[ROW8:] * cw[taps - 1:taps, cols]
+        for j in range(1, taps):
+            at = taps - 1 - j
+            acc = acc + pltpu.roll(src, j, axis=0)[ROW8:] * cw[at:at + 1, cols] * keeps[j - 1]
+        act = silu(acc).astype(BF16)
+        if i * LANES < inner:
+            xact_ref[:, cols] = act
+            xw[:, cols] = (act.astype(F32) * head_lanes(end_cols, i, head_dim)).astype(BF16)
+        else:
+            bcact_ref[:, i * LANES - inner:(i + 1) * LANES - inner] = act
+    sloc_ref[0] = send_ref[...]
     pd_ref[0] = dec_ref[...]
-    new_state = carry_lane * state[...] + dot32(bcact_ref[:, 0:n_state].T, xw[...])
-    state[...] = new_state
-    send_ref[...] = new_state
+    send_ref[...] = carry_lane * send_ref[...] + dot32(bcact_ref[:, 0:n_state].T, xw[...])
     dec_ref[...] = dec_ref[...] * carry_lane
 
 
@@ -520,7 +519,7 @@
                    full((n_state, inner)), full((1, inner))],
         out_shape=[out_of(BF16, t, inner), out_of(BF16, t, gw), out_of(F32, heads, t), out_of(F32, heads, t), out_of(F32, 1, t), out_of(F32, nt, 1, LANES),
                    out_of(F32, nt, n_state, inner), out_of(F32, nt, 1, inner), out_of(F32, n_state, inner), out_of(F32, 1, inner)],
-        scratch_shapes=[scratch(F32, q + ROW8, inner + gw), scratch(BF16, q, inner), scratch(F32, n_state, inner), scratch(F32, 1, LANES),
+        scratch_shapes=[scratch(F32, q + ROW8, inner + gw), scratch(BF16, q, inner), scratch(F32, 1, LANES),
                         scratch(jnp.int32, 1, LANES), scratch(F32, ROW8, inner + gw)],
         compiler_params=params(56),
         cost_estimate=pl.CostEstimate(flops=t * inner * gw, bytes_accessed=t * inner, transcendentals=0),
@@ -539,6 +538,8 @@
     nn = inner // nt
     tiles = CORES * nn
     pw = inner // pieces
+    parts = range(x_sem.shape[1])
+    kw = xg.shape[2] // len(parts)
 
     def tok(g):
         return rows_at(lax.rem(chip + jnp.where(g == 0, chips - 1, 1), chips) * tm, tm)
@@ -546,11 +547,14 @@
     def col(i):
         return rows_at(lax.rem(i, nn) * nt, nt)
 
-    def x_copy(g):
-        return pltpu.make_async_copy(xf_ref.at[tok(g), :], xg.at[g], x_sem.at[g])
-
-    def w_copy(i):
-        return pltpu.make_async_copy(wz_ref.at[:, col(i)], wzb.at[odd(i)], w_sem.at[odd(i)])
+    def depth(s):
+        return pl.ds(s * kw, kw)
+
+    def x_copy(g, s):
+        return pltpu.make_async_copy(xf_ref.at[tok(g), depth(s)], xg.at[g, :, depth(s)], x_sem.at[g, s])
+
+    def w_copy(i, s):
+        return pltpu.make_async_copy(wz_ref.at[depth(s), col(i)], wzb.at[odd(i), depth(s), :], w_sem.at[odd(i), s])
 
     def z_copy(i):
         return pltpu.make_async_copy(zst.at[odd(i)], z_ref.at[tok(i // nn), col(i)], z_sem.at[odd(i)])
@@ -558,9 +562,9 @@
     def hop_copy(p):
         return remote(sbuf.at[p], rbuf.at[p], s_sem.at[p], r_sem.at[p], 'sp', sp_next)
 
-    for g in PAIR:
-        x_copy(g).start()
-    w_copy(0).start()
+    for s in parts:
+        x_copy(0, s).start()
+        w_copy(0, s).start()
     ready()
 
     def body(i, carry):
@@ -590,19 +594,22 @@
         def _():
             g = i // nn
 
-            @pl.when(lax.rem(i, nn) == 0)
-            def _():
-                x_copy(g).wait()
-            w_copy(i).wait()
-
-            @pl.when(i + 1 < tiles)
-            def _():
-                w_copy(i + 1).start()
-
             @pl.when(i >= 2)
             def _():
                 z_copy(i - 2).wait()
-            zst[odd(i)] = dot32(xg[g], wzb[odd(i)]).astype(BF16)
+            res = 0.0
+            for s in parts:
+                @pl.when(lax.rem(i, nn) == 0)
+                def _(s=s):
+                    x_copy(g, s).wait()
+                w_copy(i, s).wait()
+
+                @pl.when(i + 1 < tiles)
+                def _(s=s):
+                    w_copy(i + 1, s).start()
+                pl.when(i == 1)(x_copy(1, s).start)
+                res = res + dot32(xg[g, :, depth(s)], wzb[odd(i), depth(s), :])
+            zst[odd(i)] = res.astype(BF16)
             z_copy(i).start()
         return carry
 
@@ -616,7 +623,7 @@
             hop_copy(p).wait_send()
 
 
-def z_chain(x_full, w_z, s_end, dec, chips, blocks, pieces=4, hop=2, nt=512):
+def z_chain(x_full, w_z, s_end, dec, chips, blocks, pieces=4, hop=2, nt=512, parts=4):
     t, d_model = x_full.shape
     n_state, inner = s_end.shape
     tm = t // chips
@@ -628,7 +635,7 @@
         out_specs=[ANY, VMEM],
         out_shape=[out_of(BF16, t, inner), out_of(F32, n_state, inner)],
         scratch_shapes=[scratch(BF16, 2, tm, d_model), scratch(BF16, 2, d_model, nt), scratch(BF16, 2, tm, nt), piece, piece,
-                        two, two, two, sems(pieces), sems(pieces)],
+                        sems(2, parts), sems(2, parts), two, sems(pieces), sems(pieces)],
         compiler_params=params(60, 2),
         cost_estimate=pl.CostEstimate(flops=t * inner * d_model, bytes_accessed=t * inner, transcendentals=0),
         name='z_chain',
@@ -637,21 +644,24 @@
 
 def out_kernel(chips, nb, wc, slots, zt, xact_ref, bc_ref, cum_ref, cl_ref, seg_ref, segp_ref, sloc_ref, pd_ref, sin_ref, z_ref, xf_ref, wz_ref,
                dskip_ref, nw_ref, wo_ref, wp_ref, x_ref, o_ref, recv_ref,
-               va_own, va_par, wbuf, send, rbuf, xo, xg, wzb, zb, xa, bca, sl, sbf, yoff, gated, dlane,
-               vs_sem, vr_sem, w_sem, s_sem, r_sem, l_sem, x_sem, o_sem, c_sem, z_sem):
+               va_own, va_par, wbuf, send, acc, rbuf, xo, xg, wzb, zb, xa, bca, sl, sbf, yoff, gated, dlane,
+               vs_sem, vr_sem, w_sem, s_sem, r_sem, l_sem, x_sem, o_sem, c_sem, z_sem, v_sem):
     me = lax.axis_index('tp')
     chip, core = me // CORES, odd(me)
     partner = CORES * chip + flip(core)
     chip_at = lambda d: lax.rem(chip + d, chips)
     ring = [CORES * chip_at(chips - 1) + core, CORES * chip_at(1) + core]
     q = va_own.shape[1]
-    inner = xa.shape[1]
+    inner = xa.shape[2]
     heads = cum_ref.shape[0]
     head_dim = inner // heads
     per = LANES // head_dim
-    n_state = sl.shape[0]
+    n_state = sl.shape[1]
     half_cols = nb * wc
-    steps = chips * nb * 2
+    hops = chips - 1
+    steps = hops * nb * 2
+    lag = acc.shape[1] - 1
+    depth = slots // 2
     hq = q // 2
     ready = greet([('tp', partner)] + [('tp', r) for r in ring])
 
@@ -662,22 +672,32 @@
         slot = odd(u)
         return [pltpu.make_async_copy(ref.at[:, cols_of(u)], wbuf.at[slot, i], w_sem.at[slot, i]) for i, ref in enumerate((wo_ref, wp_ref))]
 
+    def place(n):
+        return chip_at(jnp.where(n == 0, chips - 1, jnp.where(n == hops, 0, n)))
+
+    def parity(i):
+        return jnp.where(i == 0, flip(core), core)
+
+    def load(n, i):
+        c = CORES * place(n) + parity(i)
+        at = rows_at(c * q, q)
+        return [pltpu.make_async_copy(xact_ref.at[at, :], xa.at[i], c_sem.at[i, 0]), pltpu.make_async_copy(bc_ref.at[at, :], bca.at[i], c_sem.at[i, 1]),
+                pltpu.make_async_copy(sloc_ref.at[c], sl.at[i], c_sem.at[i, 2]), pltpu.make_async_copy(z_ref.at[at, :], zb.at[parity(i)], c_sem.at[i, 3])]
+
+    for i in PAIR:
+        for cp in load(0, i):
+            cp.start()
     for cp in w_copies(0):
         cp.start()
     x_copy = pltpu.make_async_copy(x_ref, xo, x_sem)
-    x_copy.start()
     dlane[...] = expand_heads(dskip_ref[...], head_dim)
     ready()
 
     def swap(n, j):
         return remote(va_own.at[chips + odd(n)], va_par.at[j], vs_sem.at[n], vr_sem.at[n], 'tp', partner)
 
-    def mix(c, zrow, tgt):
+    def mix(c, i, tgt):
         at = rows_at(c * q, q)
-        copies = [pltpu.make_async_copy(xact_ref.at[at, :], xa, c_sem.at[0]), pltpu.make_async_copy(bc_ref.at[at, :], bca, c_sem.at[1]),
-                  pltpu.make_async_copy(sloc_ref.at[c], sl, c_sem.at[2])]
-        for cp in copies:
-            cp.start()
         seg_row = seg_ref[:, at]
         seg_prev = segp_ref[c][:, LANES - 1:]
         seg_rows = jnp.broadcast_to(seg_row, (q, q))
@@ -687,20 +707,18 @@
         cl = cl_ref[:, at]
         cum_cols = cum.T
         in_cols = jnp.where(seg_row == seg_prev, jnp.exp2(cum), 0.0).T
-        for cp in copies:
-            cp.wait()
-        sbf[...] = (sl[...] + pd_ref[c] * sin_ref[...]).astype(BF16)
-        c_act = bca[:, n_state:]
-        scores = lax.dot_general(c_act, bca[:, 0:n_state], (((1,), (1,)), ((), ())), preferred_element_type=F32)
+        sbf[...] = (sl[i] + pd_ref[c] * sin_ref[...]).astype(BF16)
+        c_act = bca[i, :, n_state:]
+        scores = lax.dot_general(c_act, bca[i, :, 0:n_state], (((1,), (1,)), ((), ())), preferred_element_type=F32)
         yoff[...] = dot32(c_act, sbf[...])
         lane = lax.broadcasted_iota(jnp.int32, (q, LANES), 1) // head_dim
         sq = jnp.zeros((q, LANES), F32)
-        for i in range(inner // LANES):
-            cols = slice(i * LANES, (i + 1) * LANES)
-            x_f = xa[:, cols].astype(F32)
+        for m in range(inner // LANES):
+            cols = slice(m * LANES, (m + 1) * LANES)
+            x_f = xa[i, :, cols].astype(F32)
             tops, bots = [], []
             for j in range(per):
-                h = i * per + j
+                h = m * per + j
                 x_h = jnp.where(lane == j, x_f, 0.0).astype(BF16)
                 ccol, crow = cum_cols[:, h:h + 1], cl[h:h + 1, :]
                 m_top = jnp.exp2(ccol[0:hq] + bias[0:hq, 0:hq] - crow[:, 0:hq]) * scores[0:hq, 0:hq]
@@ -708,32 +726,29 @@
                 tops.append(dot32(m_top.astype(BF16), x_h[0:hq]))
                 bots.append(dot32(m_bot.astype(BF16), x_h))
             y = jnp.concatenate([sum(tops), sum(bots)], axis=0)
-            y = y + yoff[:, cols] * head_lanes(in_cols, i, head_dim) + dlane[:, cols] * x_f
-            v = y * silu(zb[zrow, :, cols].astype(F32))
+            y = y + yoff[:, cols] * head_lanes(in_cols, m, head_dim) + dlane[:, cols] * x_f
+            v = y * silu(zb[parity(i), :, cols].astype(F32))
             gated[:, cols] = v
             sq = sq + v * v
         inv = lax.rsqrt(jnp.sum(sq, axis=1, keepdims=True) * (1.0 / inner) + NORM_EPS)
         inv = jnp.broadcast_to(inv, (q, LANES))
-        for i in range(inner // LANES):
-            cols = slice(i * LANES, (i + 1) * LANES)
-            va_own[tgt, :, cols] = (gated[:, cols] * inv * nw_ref[:, cols].astype(F32)).astype(BF16)
+        for m in range(inner // LANES):
+            cols = slice(m * LANES, (m + 1) * LANES)
+            va_own[tgt, :, cols] = (gated[:, cols] * inv * nw_ref[m:m + 1, :].astype(F32)).astype(BF16)
 
     def prep(n):
-        j = chip_at(jnp.where(n == 0, chips - 1, jnp.where(n == 3, 0, n)))
+        j = place(n)
         tok = rows_at(j * (CORES * q), CORES * q)
 
-        @pl.when(n < 2)
-        def _():
-            for p in PAIR:
-                pltpu.make_async_copy(z_ref.at[rows_at((CORES * j + p) * q, q), :], zb.at[p], c_sem.at[p]).start()
-            for p in PAIR:
-                pltpu.make_async_copy(z_ref.at[rows_at((CORES * j + p) * q, q), :], zb.at[p], c_sem.at[p]).wait()
-
         @pl.when(n >= 2)
         def _():
+            for i in PAIR:
+                for cp in load(n, i)[:3]:
+                    cp.start()
+
             def wz_copy(m):
                 return pltpu.make_async_copy(wz_ref.at[:, rows_at(m * zt, zt)], wzb.at[odd(m)], z_sem.at[odd(m)])
-            rows_copy = pltpu.make_async_copy(xf_ref.at[tok, :], xg, c_sem.at[0])
+            rows_copy = pltpu.make_async_copy(xf_ref.at[tok, :], xg, v_sem)
             rows_copy.start()
             wz_copy(0).start()
             rows_copy.wait()
@@ -753,8 +768,18 @@
             swap(n - 2, j).wait_send()
 
         def chunk(i, carry):
-            par = jnp.where(i == 0, flip(core), core)
-            mix(CORES * j + par, par, jnp.where(i == 0, chips + odd(n), j))
+            for cp in load(n, i)[:3]:
+                cp.wait()
+
+            @pl.when(n < 2)
+            def _():
+                load(n, i)[3].wait()
+            mix(CORES * j + parity(i), i, jnp.where(i == 0, chips + odd(n), j))
+
+            @pl.when(n == 0)
+            def _():
+                for cp in load(1, i):
+                    cp.start()
 
             @pl.when(i == 0)
             def _():
@@ -777,13 +802,23 @@
         cols = rows_at(d * half_cols + b * wc, wc)
         return pltpu.make_async_copy(xo.at[:, cols], o_ref.at[:, cols], o_sem.at[d, b])
 
+    def product(dest, slot):
+        return dot32(va_own[dest], wbuf[slot, 0]) + dot32(va_par[dest], wbuf[slot, 1])
+
+    def finish(d, b):
+        fetch(d, (hops - 1) * nb + b)
+        cols = rows_at(d * half_cols + b * wc, wc)
+        xo[:, cols] = (xo[:, cols].astype(F32) + (acc[d, lax.rem(b, lag + 1)] + rbuf[...])).astype(BF16)
+        o_copy(d, b).start()
+
     def body(u, carry):
         d = odd(u)
         k = u // (2 * nb)
         b = lax.rem(u // 2, nb)
         unit = k * nb + b
-
-        @pl.when((u < 2) | ((b == 0) & (d == 0) & (k < chips - 1)))
+        ending = k == hops - 1
+
+        @pl.when((u < 2) | ((b == 0) & (d == 0)))
         def _():
             prep(jnp.where(u < 2, u, k + 1))
         dest = chip_at(jnp.where(d == 0, 2 * chips - 1 - k, 1 + k))
@@ -794,47 +829,59 @@
         def _():
             for cp in w_copies(u + 1):
                 cp.start()
-        part = dot32(va_own[dest], wbuf[odd(u), 0]) + dot32(va_par[dest], wbuf[odd(u), 1])
-
-        @pl.when(k < chips - 1)
-        def _():
-            slot = lax.rem(unit, slots)
-
-            @pl.when(unit >= slots)
+
+        @pl.when(u == 2)
+        def _():
+            x_copy.start()
+        part = product(dest, d)
+        slot = lax.rem(unit, slots)
+
+        @pl.when((unit >= slots) & (flip(ending) | (b < slots - depth)))
+        def _():
+            ring_copy(d, unit - slots).wait_send()
+
+        @pl.when(ending)
+        def _():
+            ring_copy(d, unit - depth).wait_send()
+
+        @pl.when(k == 0)
+        def _():
+            send[d, slot] = part
+
+        @pl.when(k > 0)
+        def _():
+            fetch(d, unit - nb)
+            send[d, slot] = part + rbuf[...]
+        ring_copy(d, unit).start()
+
+        @pl.when(ending)
+        def _():
+            acc[d, lax.rem(b, lag + 1)] = product(chip, d)
+
+            @pl.when(b == 0)
             def _():
-                ring_copy(d, unit - slots).wait_send()
-
-            @pl.when(k == 0)
+                pl.when(d == 0)(x_copy.wait)
+
+            @pl.when(b >= lag)
             def _():
-                send[d, slot] = part
-
-            @pl.when(k > 0)
-            def _():
-                fetch(d, unit - nb)
-                send[d, slot] = part + rbuf[...]
-            ring_copy(d, unit).start()
-
-        @pl.when(k == chips - 1)
-        def _():
-            @pl.when((b == 0) & (d == 0))
-            def _():
-                x_copy.wait()
-            fetch(d, unit - nb)
-            cols = cols_of(u)
-            xo[:, cols] = (xo[:, cols].astype(F32) + (part + rbuf[...])).astype(BF16)
-            o_copy(d, b).start()
+                finish(d, b - lag)
         return carry
 
     lax.fori_loop(0, steps, body, 0)
+
+    def tail(i, carry):
+        finish(odd(i), nb - lag + i // 2)
+        return carry
 
     def drain(i, carry):
         o_copy(odd(i), i // 2).wait()
         return carry
 
     def drain_send(i, carry):
-        ring_copy(odd(i), (chips - 1) * nb - slots + i // 2).wait_send()
+        ring_copy(odd(i), hops * nb - depth + i // 2).wait_send()
         return carry
-    lax.fori_loop(0, 2 * slots, drain_send, 0)
+    lax.fori_loop(0, 2 * lag, tail, 0)
+    lax.fori_loop(0, 2 * depth, drain_send, 0)
     for n in PAIR:
         swap(2 + n, chip).wait_send()
     lax.fori_loop(0, 2 * nb, drain, 0)
@@ -852,11 +899,11 @@
         in_specs=[ANY, ANY, VMEM, VMEM, VMEM, VMEM, ANY, VMEM, VMEM, ANY, ANY, ANY, VMEM, VMEM, ANY, ANY, ANY],
         out_specs=[ANY, ANY],
         out_shape=[out_of(BF16, rows, d_model), out_of(F32, 2, units, rows, wc)],
-        scratch_shapes=[scratch(BF16, chips + 2, rows, inner), scratch(BF16, chips, rows, inner), scratch(BF16, 2, 2, inner, wc), scratch(F32, 2, slots, rows, wc),
+        scratch_shapes=[scratch(BF16, chips + 2, rows, inner), scratch(BF16, chips, rows, inner), scratch(BF16, 2, 2, inner, wc), scratch(F32, 2, slots, rows, wc), scratch(F32, 2, slots, rows, wc),
                         scratch(F32, rows, wc), scratch(BF16, rows, d_model), scratch(BF16, CORES * rows, d_model), scratch(BF16, 2, d_model, zt),
-                        scratch(BF16, CORES, rows, inner), scratch(BF16, rows, inner), scratch(BF16, rows, gw), scratch(F32, n_state, inner),
+                        scratch(BF16, CORES, rows, inner), scratch(BF16, 2, rows, inner), scratch(BF16, 2, rows, gw), scratch(F32, 2, n_state, inner),
                         scratch(BF16, n_state, inner), scratch(F32, rows, inner), scratch(F32, rows, inner), scratch(F32, 1, inner),
-                        sems(chips), sems(chips), sems(2, 2), sems(2, slots), sems(2, units), DMA, DMA, sems(2, nb), sems(3), sems(2)],
+                        sems(chips), sems(chips), sems(2, 2), sems(2, slots), sems(2, units), DMA, DMA, sems(2, nb), sems(2, 4), sems(2), DMA],
         compiler_params=params(63, 1),
         cost_estimate=pl.CostEstimate(flops=2 * t * inner * d_model, bytes_accessed=t * d_model, transcendentals=0),
         name='out_proj_scatter',
@@ -865,11 +912,12 @@
 
 def layer(x_loc, seg_loc, w_zx, w_bc, w_dt, conv_x, conv_bc, bias_x, bias_bc, a_log, dt_bias, d_skip, norm_w, w_out, chips, blocks):
     rows = x_loc.shape[0]
+    tiled = lambda v: v.reshape(v.shape[0] // LANES, LANES)
     x_full, x_pre, small, w_z, w_par, seg, seg_tail, tail_x, tail_b = gather_proj(x_loc, w_zx, w_bc, w_dt.T, w_out, seg_loc[None], chips, blocks)
     x_act, bc_act, cum, cl, seg_row, seg_prev, sloc, pd, s_end, dec = phase_a(
-        x_pre, small, seg, seg_tail, tail_x, tail_b, conv_x, conv_bc, bias_x[None], bias_bc, a_log[None], dt_bias[None], rows)
+        x_pre, small, seg, seg_tail, tail_x, tail_b, conv_x, conv_bc, tiled(bias_x), bias_bc, a_log[None], dt_bias[None], rows)
     z_arr, s_in = z_chain(x_full, w_z, s_end, dec, chips, blocks)
-    return out_proj_scatter(x_act, bc_act, cum, cl, seg_row, seg_prev, sloc, pd, s_in, z_arr, x_full, w_z, d_skip[None], norm_w[None], w_out, w_par, x_loc, chips)
+    return out_proj_scatter(x_act, bc_act, cum, cl, seg_row, seg_prev, sloc, pd, s_in, z_arr, x_full, w_z, d_skip[None], tiled(norm_w), w_out, w_par, x_loc, chips)
 
 
 def solution(mesh):

time: 561 us -> 544 us (0.970)
  Pallas kernels: 552 us -> 538 us
    pallas_call x1, Pallas kernels: 307 us -> 298 us  [out_proj_scatter(): pl.pallas_call(functools.partial(out_kernel, chips, nb, wc, slots, zt), i...]
where the time goes in v3:
time: 544 us; the launch traced here: 542 us
  Pallas kernels  538 us (99%)
    pallas_call x1, Pallas kernels, out_proj_scatter(): pl.pallas_call(functools.partial(out_kernel, chips, nb, wc, slots, zt), i...  298 us
    pallas_call x1, Pallas kernels, gather_proj(): pl.pallas_call(functools.partial(gather_kernel, chips, blocks, kb, nb, su...  164 us
    pallas_call x1, Pallas kernels, z_chain(): pl.pallas_call(functools.partial(chain_kernel, chips, blocks, pieces, hop...  45.7 us
    pallas_call x1, Pallas kernels, phase_a(): pl.pallas_call(functools.partial(phase_a_kernel, q), grid=(nt,), in_specs...  29.5 us

profile of v3, /device:TPU:97, one launch (start us, length us, event | category | flops | bytes accessed | tf_op | source)
XLA Modules:
  0.0 542.3 jit_solution(14949068209406761307)
XLA Ops:
  0.0 164.3 %gather_proj.1 = (bf16[2048,8192]{1,0:T(8,128)(2,1)}, bf16[2048,2048]{1,0:T(8,128)(2,1)}, bf16[2048,384]{1,0:T(8,128)(2,1)}, bf16[8192,2048]{1,0:T(8,128)(2,1)},...) custom-call(bf16[256,8192]{1,0:T(8,128)(2,1)} %x_ref.3, ...), custom_call_target="tpu_custom_call" | custom-call | flops 34359738368 | bytes 4194304 | tf_op jit(solution)/shard_map/gather_proj/pallas_call | solution.py:403
  164.3 29.5 %phase_a.1 = (bf16[2048,2048]{1,0:T(8,128)(2,1)}, bf16[2048,256]{1,0:T(8,128)(2,1)}, f32[32,2048]{1,0:T(8,128)}, f32[32,2048]{1,0:T(8,128)}, f32[1,2048]{1,0:T(1...) custom-call(bf16[2048,2048]{1,0:T(8,128)(2,1)} %get-tuple-element.27, ...), custom_call_target="tpu_custom_call" | custom-call | flops 1073741824 | bytes 4194304 | tf_op jit(solution)/shard_map/phase_a/pallas_call | solution.py:514
  193.8 45.7 %z_chain.1 = (bf16[2048,2048]{1,0:T(8,128)(2,1)}, f32[128,2048]{1,0:T(8,128)}) custom-call(bf16[2048,8192]{1,0:T(8,128)(2,1)} %get-tuple-element.41.xf_ref, bf16[8192,2048]{1,0:T(8,128)(2,1)} %get-tuple-element.42.wz_ref, f32[128,2048]{1,0:T(8,128)} %get-tuple-element.43.send_ref, f32[1,2048]{1,0:T(1,128)} %get-tuple-element.44.dec_ref), custom_call_target="tpu_custom_call" | custom-call | flops 34359738368 | bytes 4194304 | tf_op jit(solution)/shard_map/z_chain/pallas_call | solution.py:632
  239.5 298.1 %out_proj_scatter.1 = (bf16[256,8192]{1,0:T(8,128)(2,1)}, f32[2,24,256,512]{3,2,1,0:T(8,128)}) custom-call(bf16[2048,2048]{1,0:T(8,128)(2,1)} %get-tuple-element.33.xact_ref, bf16[2048,256]{1,0:T(8,128)(2,1)} %get-tuple-element.34.bc_ref, f32[32,2048]{1,0:T(8,128)} %get-tuple-element.35.cum_ref, f32[32,2048]{1,0:T(8,128)} %get-tuple-element.36.cl_ref, ...), custom_call_target="tpu_custom_call" | custom-call | flops 68719476736 | bytes 16777216 | tf_op jit(solution)/shard_map/out_proj_scatter/pallas_call | solution.py:897
  537.6 4.6 copy.16

commit v4 on v3

--- a/solution.py
+++ b/solution.py
@@ -18,6 +18,7 @@
 LANES = 128
 ROW8 = 8
 CORES = 2
+DIRS = 2
 PAIR = range(2)
 ANY = pl.BlockSpec(memory_space=pl.ANY)
 VMEM = pl.BlockSpec(memory_space=pltpu.VMEM)
@@ -107,7 +108,7 @@
     chip, core = me // CORES, odd(me)
     partner = CORES * chip + flip(core)
     near = [lax.rem(chip + chips - 1, chips), lax.rem(chip + 1, chips)]
-    far = lax.rem(chip + chips // 2, chips)
+    far = lax.rem(chip + chips // CORES, chips)
     ring = [CORES * c + core for c in near]
     sp_next = lax.rem(blk_id + 1, blocks)
     n_tp = CORES * chips
@@ -119,16 +120,16 @@
     n_state = bblk.shape[3]
     nk = d_model // kb
     nblk = nk * (inner // nb)
-    opp = 2 + quarters
-    last = opp + quarters // 2 - 1
+    opp = CORES + quarters
+    last = opp + quarters // CORES - 1
     ready = greet([('tp', lax.rem(me + d, n_tp)) for d in range(1, n_tp)] + [('sp', sp_next), ('sp', lax.rem(blk_id + blocks - 1, blocks))])
 
     def row_of(lv, b):
         side = odd(b)
-        other = jnp.where(lv < 2, lv, b // 2)
+        other = jnp.where(lv < CORES, lv, b // CORES)
         cc = jnp.where(other == 1, flip(core), core)
-        ch = jnp.where(lv < 2, chip, jnp.where(lv >= opp, far, jnp.where(side == 0, near[0], near[1])))
-        q = jnp.where(lv < 2, b, jnp.where(lv >= opp, side * (quarters // 2) + lv - opp, lv - 2))
+        ch = jnp.where(lv < CORES, chip, jnp.where(lv >= opp, far, jnp.where(side == 0, near[0], near[1])))
+        q = jnp.where(lv < CORES, b, jnp.where(lv >= opp, side * (quarters // CORES) + lv - opp, lv - CORES))
         return (CORES * ch + cc) * rows + q * qr
 
     def full_rows(lv, b, size=qr):
@@ -159,7 +160,7 @@
     ready()
 
     def own_send(q, to):
-        return remote(x_ref.at[rows_at(q * qr, qr), :], full_rows(0, q), so_sem.at[to, q], ra_sem.at[2 + q, flip(to)], 'tp', ring[to])
+        return remote(x_ref.at[rows_at(q * qr, qr), :], full_rows(0, q), so_sem.at[to, q], ra_sem.at[CORES + q, flip(to)], 'tp', ring[to])
 
     own_pair = remote(x_ref, full_rows(0, 0, rows), sd_sem.at[1, 0], rd_sem.at[1, 0], 'tp', partner)
 
@@ -168,7 +169,7 @@
 
     def forward(lv, to):
         side = flip(to)
-        h = lax.rem(lv - 2, quarters // 2)
+        h = lax.rem(lv - CORES, quarters // CORES)
         dst_sem = ra_sem.at[opp + h, side]
         return remote(full_rows(lv, side), full_rows(lv, side), sf_sem.at[to, h], dst_sem, 'tp', ring[to])
 
@@ -176,7 +177,7 @@
         return remote(full_rows(lv, side), full_rows(lv, side), so_sem.at[0, 0], ra_sem.at[lv, side], 'tp', ring[0])
 
     def pair_arrival(lv, side):
-        ref = full_rows(lv, 2 + side)
+        ref = full_rows(lv, CORES + side)
         return remote(ref, ref, sd_sem.at[1, 0], rd_sem.at[lv, side], 'tp', partner)
 
     pair_own_arrival = remote(full_rows(1, 0, rows), full_rows(1, 0, rows), sd_sem.at[1, 0], rd_sem.at[1, 0], 'tp', partner)
@@ -229,7 +230,7 @@
             for g in PAIR:
                 wsm[at, g * n_state:(g + 1) * n_state] = part[g]
             wd = jnp.concatenate([wdt[:, at].astype(F32), jnp.zeros((LANES - heads, sub), F32)], axis=0)
-            wsm[at, 2 * n_state:] = wd.T.astype(BF16)
+            wsm[at, CORES * n_state:] = wd.T.astype(BF16)
             return carry2
         return lax.fori_loop(0, kb // sub, inner_body, carry)
     lax.fori_loop(0, nk, small_body, 0)
@@ -238,9 +239,9 @@
         slot = lax.rem(i, blk.shape[0])
         blk_copy(i).wait()
 
-        @pl.when(i >= 2)
-        def _():
-            z_copy(i - 2).wait()
+        @pl.when(i >= CORES)
+        def _():
+            z_copy(i - CORES).wait()
         kk = lax.rem(i, nk) * kb
 
         def inner_body(s, carry2):
@@ -272,7 +273,7 @@
         return pltpu.make_async_copy(full_rows(lv, b), xg.at[odd(lv), rows_at(b * qr, qr), :], xl_sem.at[odd(lv), b])
 
     def take(lv):
-        @pl.when(lv >= 2)
+        @pl.when(lv >= CORES)
         def _():
             for side in PAIR:
                 arrival(lv, side).wait_recv()
@@ -283,7 +284,7 @@
         def _():
             pair_own_arrival.wait_recv()
 
-        @pl.when(lv >= 2)
+        @pl.when(lv >= CORES)
         def _():
             for side in PAIR:
                 pair_arrival(lv, side).wait_recv()
@@ -300,16 +301,16 @@
         return res
 
     early = opp - 1
-    cut = 2 + quarters // 2
+    cut = CORES + quarters // CORES
 
     def feed(lv):
         @pl.when(lv == 1)
         def _():
             send_quarter(quarters - 1)
-        for h in range(quarters // 2):
-            @pl.when(lv == 3 + 2 * h)
+        for h in range(quarters // CORES):
+            @pl.when(lv == 3 + CORES * h)
             def _(h=h):
-                forward(2 + h, 1).start()
+                forward(CORES + h, 1).start()
                 forward(cut + h, 0).start()
 
     def round_body(lv, carry):
@@ -328,13 +329,13 @@
         def _():
             take(lv + 1)
 
-        @pl.when(lv >= 2)
-        def _():
-            for cp in out_copies(lv - 2):
+        @pl.when(lv >= CORES)
+        def _():
+            for cp in out_copies(lv - CORES):
                 cp.wait()
 
         def dots(n, carry2):
-            @pl.when(n == inner // nt // 2)
+            @pl.when(n == inner // nt // CORES)
             def _():
                 feed(lv)
 
@@ -368,7 +369,7 @@
 
     @pl.when(halo_lv == last)
     def _():
-        for cp in halo_copies(last % 2):
+        for cp in halo_copies(last % CORES):
             cp.wait_send()
     for cp in halo_copies(0):
         cp.wait_recv()
@@ -384,33 +385,33 @@
     for to in PAIR:
         for q in range(quarters):
             own_send(q, to).wait_send()
-        for h in range(quarters // 2):
-            forward(2 + h, to).wait_send()
-    for lv in range(2, last + 1):
+        for h in range(quarters // CORES):
+            forward(CORES + h, to).wait_send()
+    for lv in range(CORES, last + 1):
         for side in PAIR:
             pair_send(lv, side).wait_send()
 
 
 def gather_proj(x_loc, w_zx, w_bc, w_dt_t, w_out, seg, chips, blocks, kb=2048, nb=256, sub=256, nt=512, quarters=4, pace=12):
     rows, d_model = x_loc.shape
-    inner, n_state, heads = w_zx.shape[2], w_bc.shape[2], w_dt_t.shape[0]
+    inner, n_state, heads = w_zx.shape[CORES], w_bc.shape[CORES], w_dt_t.shape[0]
     n_tp = CORES * chips
     t = rows * n_tp
     small = CORES * n_state + LANES
-    lv = CORES + quarters + quarters // 2
+    lv = CORES + quarters + quarters // CORES
     halo = 16
-    two = sems(2)
+    two = sems(CORES)
     return pl.pallas_call(
         functools.partial(gather_kernel, chips, blocks, kb, nb, sub, nt, pace),
         in_specs=[ANY] * 6,
         out_specs=[ANY] * 9,
         out_shape=[out_of(BF16, t, d_model), out_of(BF16, t, inner), out_of(BF16, t, small), out_of(BF16, d_model, inner), out_of(BF16, *w_out.shape),
                    out_of(jnp.int32, 1, t), out_of(jnp.int32, 1, LANES), out_of(BF16, halo, inner), out_of(BF16, halo, small)],
-        scratch_shapes=[scratch(BF16, d_model, inner), scratch(BF16, d_model, small), scratch(BF16, 2, rows, d_model),
-                        scratch(BF16, 2, rows, inner), scratch(BF16, 2, rows, small), scratch(BF16, 3, kb, CORES, nb),
-                        scratch(BF16, 2, kb, CORES, n_state), scratch(BF16, 2, kb, nb), scratch(BF16, heads, d_model),
-                        sems(lv, 2), sems(lv, 2), sems(2, quarters), sems(2, quarters), sems(lv, 2), sems(2, quarters), two, sems(3), two, two, DMA,
-                        sems(2, quarters), sems(2, quarters), two, sems(n_tp), sems(n_tp), two, two, two],
+        scratch_shapes=[scratch(BF16, d_model, inner), scratch(BF16, d_model, small), scratch(BF16, CORES, rows, d_model),
+                        scratch(BF16, CORES, rows, inner), scratch(BF16, CORES, rows, small), scratch(BF16, 3, kb, CORES, nb),
+                        scratch(BF16, CORES, kb, CORES, n_state), scratch(BF16, CORES, kb, nb), scratch(BF16, heads, d_model),
+                        sems(lv, CORES), sems(lv, CORES), sems(CORES, quarters), sems(CORES, quarters), sems(lv, CORES), sems(CORES, quarters), two, sems(3), two, two, DMA,
+                        sems(CORES, quarters), sems(CORES, quarters), two, sems(n_tp), sems(n_tp), two, two, two],
         compiler_params=params(63, 0),
         cost_estimate=pl.CostEstimate(flops=t * inner * d_model, bytes_accessed=t * inner, transcendentals=0),
         name='gather_proj',
@@ -527,7 +528,7 @@
     )(x_pre, small, seg, *rest)
 
 
-def chain_kernel(chips, blocks, pieces, hop, nt, xf_ref, wz_ref, send_ref, dec_ref, z_ref, sin_ref,
+def chain_kernel(chips, blocks, pieces, hop, gap, nt, xf_ref, wz_ref, send_ref, dec_ref, z_ref, sin_ref,
                  xg, wzb, zst, sbuf, rbuf, x_sem, w_sem, z_sem, s_sem, r_sem):
     chip = lax.axis_index('tp') // CORES
     blk_id = lax.axis_index('sp')
@@ -536,13 +537,13 @@
     n_state, inner = send_ref.shape
     tm = xg.shape[1]
     nn = inner // nt
-    tiles = CORES * nn
+    tiles = nn + nn // CORES
     pw = inner // pieces
     parts = range(x_sem.shape[1])
     kw = xg.shape[2] // len(parts)
 
     def tok(g):
-        return rows_at(lax.rem(chip + jnp.where(g == 0, chips - 1, 1), chips) * tm, tm)
+        return rows_at(lax.rem(chip + jnp.where(g == 0, chips // 2, 1), chips) * tm, tm)
 
     def col(i):
         return rows_at(lax.rem(i, nn) * nt, nt)
@@ -567,10 +568,11 @@
         w_copy(0, s).start()
     ready()
 
-    def body(i, carry):
-        p = i - hop * blk_id
-
-        @pl.when((p >= 0) & (p < pieces))
+    def pass_on(j):
+        lead = j - hop * blk_id
+        p = lead // gap
+
+        @pl.when((lead >= 0) & (lax.rem(lead, gap) == 0) & (p < pieces))
         def _():
             cols = rows_at(p * pw, pw)
 
@@ -590,30 +592,32 @@
             def _():
                 hop_copy(p).start()
 
-        @pl.when(i < tiles)
-        def _():
-            g = i // nn
-
-            @pl.when(i >= 2)
-            def _():
-                z_copy(i - 2).wait()
-            res = 0.0
-            for s in parts:
-                @pl.when(lax.rem(i, nn) == 0)
-                def _(s=s):
-                    x_copy(g, s).wait()
-                w_copy(i, s).wait()
-
-                @pl.when(i + 1 < tiles)
-                def _(s=s):
-                    w_copy(i + 1, s).start()
-                pl.when(i == 1)(x_copy(1, s).start)
-                res = res + dot32(xg[g, :, depth(s)], wzb[odd(i), depth(s), :])
-            zst[odd(i)] = res.astype(BF16)
-            z_copy(i).start()
-        return carry
-
-    lax.fori_loop(0, max(tiles, hop * (blocks - 1) + pieces), body, 0)
+    def tile(i):
+        g = i // nn
+
+        @pl.when(i >= 2)
+        def _():
+            z_copy(i - 2).wait()
+        res = 0.0
+        for s in parts:
+            @pl.when(lax.rem(i, nn) == 0)
+            def _(s=s):
+                x_copy(g, s).wait()
+            w_copy(i, s).wait()
+
+            @pl.when(i + 1 < tiles)
+            def _(s=s):
+                w_copy(i + 1, s).start()
+            pl.when(i == 1)(x_copy(1, s).start)
+            pass_on(i * len(parts) + s)
+            res = res + dot32(xg[g, :, depth(s)], wzb[odd(i), depth(s), :])
+        zst[odd(i)] = res.astype(BF16)
+        z_copy(i).start()
+
+    steps = hop * (blocks - 1) + gap * (pieces - 1) + 1
+    lax.fori_loop(0, tiles, lambda i, carry: (tile(i), carry)[1], 0)
+    lax.fori_loop(tiles * len(parts), steps, lambda j, carry: (pass_on(j), carry)[1], 0)
+
     for i in PAIR:
         z_copy(tiles - 1 - i).wait()
 
@@ -623,14 +627,14 @@
             hop_copy(p).wait_send()
 
 
-def z_chain(x_full, w_z, s_end, dec, chips, blocks, pieces=4, hop=2, nt=512, parts=4):
+def z_chain(x_full, w_z, s_end, dec, chips, blocks, pieces=8, hop=5, gap=2, nt=512, parts=4):
     t, d_model = x_full.shape
     n_state, inner = s_end.shape
     tm = t // chips
     piece = scratch(F32, pieces, n_state, inner // pieces)
     two = sems(2)
     return pl.pallas_call(
-        functools.partial(chain_kernel, chips, blocks, pieces, hop, nt),
+        functools.partial(chain_kernel, chips, blocks, pieces, hop, gap, nt),
         in_specs=[ANY, ANY, VMEM, VMEM],
         out_specs=[ANY, VMEM],
         out_shape=[out_of(BF16, t, inner), out_of(F32, n_state, inner)],
@@ -642,7 +646,7 @@
     )(x_full, w_z, s_end, dec)
 
 
-def out_kernel(chips, nb, wc, slots, zt, xact_ref, bc_ref, cum_ref, cl_ref, seg_ref, segp_ref, sloc_ref, pd_ref, sin_ref, z_ref, xf_ref, wz_ref,
+def out_kernel(chips, nb, wc, slots, zt, zlast, xact_ref, bc_ref, cum_ref, cl_ref, seg_ref, segp_ref, sloc_ref, pd_ref, sin_ref, z_ref, xf_ref, wz_ref,
                dskip_ref, nw_ref, wo_ref, wp_ref, x_ref, o_ref, recv_ref,
                va_own, va_par, wbuf, send, acc, rbuf, xo, xg, wzb, zb, xa, bca, sl, sbf, yoff, gated, dlane,
                vs_sem, vr_sem, w_sem, s_sem, r_sem, l_sem, x_sem, o_sem, c_sem, z_sem, v_sem):
@@ -652,28 +656,30 @@
     chip_at = lambda d: lax.rem(chip + d, chips)
     ring = [CORES * chip_at(chips - 1) + core, CORES * chip_at(1) + core]
     q = va_own.shape[1]
-    inner = xa.shape[2]
+    inner = xa.shape[DIRS]
     heads = cum_ref.shape[0]
     head_dim = inner // heads
     per = LANES // head_dim
     n_state = sl.shape[1]
     half_cols = nb * wc
     hops = chips - 1
-    steps = hops * nb * 2
+    steps = hops * nb * DIRS
     lag = acc.shape[1] - 1
-    depth = slots // 2
-    hq = q // 2
+    depth = slots // DIRS
+    hq = q // DIRS
     ready = greet([('tp', partner)] + [('tp', r) for r in ring])
 
     def cols_of(u):
-        return rows_at(odd(u) * half_cols + lax.rem(u // 2, nb) * wc, wc)
+        d = odd(u)
+        side = jnp.where(u < DIRS * nb * (hops - 1), d, flip(d))
+        return rows_at(side * half_cols + lax.rem(u // DIRS, nb) * wc, wc)
 
     def w_copies(u):
         slot = odd(u)
         return [pltpu.make_async_copy(ref.at[:, cols_of(u)], wbuf.at[slot, i], w_sem.at[slot, i]) for i, ref in enumerate((wo_ref, wp_ref))]
 
     def place(n):
-        return chip_at(jnp.where(n == 0, chips - 1, jnp.where(n == hops, 0, n)))
+        return chip_at(jnp.where(n == 0, chips // DIRS, jnp.where(n == 1, 1, jnp.where(n == DIRS, chips - 1, 0))))
 
     def parity(i):
         return jnp.where(i == 0, flip(core), core)
@@ -682,7 +688,7 @@
         c = CORES * place(n) + parity(i)
         at = rows_at(c * q, q)
         return [pltpu.make_async_copy(xact_ref.at[at, :], xa.at[i], c_sem.at[i, 0]), pltpu.make_async_copy(bc_ref.at[at, :], bca.at[i], c_sem.at[i, 1]),
-                pltpu.make_async_copy(sloc_ref.at[c], sl.at[i], c_sem.at[i, 2]), pltpu.make_async_copy(z_ref.at[at, :], zb.at[parity(i)], c_sem.at[i, 3])]
+                pltpu.make_async_copy(sloc_ref.at[c], sl.at[i], c_sem.at[i, DIRS]), pltpu.make_async_copy(z_ref.at[at, :], zb.at[parity(i)], c_sem.at[i, 3])]
 
     for i in PAIR:
         for cp in load(0, i):
@@ -740,17 +746,26 @@
         j = place(n)
         tok = rows_at(j * (CORES * q), CORES * q)
 
-        @pl.when(n >= 2)
+        @pl.when(n >= DIRS)
         def _():
             for i in PAIR:
                 for cp in load(n, i)[:3]:
                     cp.start()
+
+        @pl.when(n < DIRS)
+        def _():
+            for i in PAIR:
+                load(n, i)[3].wait()
+
+        @pl.when(n >= 1)
+        def _():
+            first = jnp.where(n == 1, (inner - zlast) // zt, 0)
 
             def wz_copy(m):
                 return pltpu.make_async_copy(wz_ref.at[:, rows_at(m * zt, zt)], wzb.at[odd(m)], z_sem.at[odd(m)])
             rows_copy = pltpu.make_async_copy(xf_ref.at[tok, :], xg, v_sem)
             rows_copy.start()
-            wz_copy(0).start()
+            wz_copy(first).start()
             rows_copy.wait()
 
             def z_body(m, carry):
@@ -763,17 +778,15 @@
                 for p in PAIR:
                     zb[p, :, rows_at(m * zt, zt)] = res[p * q:(p + 1) * q]
                 return carry
-            lax.fori_loop(0, inner // zt, z_body, 0)
-
-            swap(n - 2, j).wait_send()
+            lax.fori_loop(first, inner // zt, z_body, 0)
+
+        @pl.when(n >= DIRS)
+        def _():
+            swap(n - DIRS, j).wait_send()
 
         def chunk(i, carry):
             for cp in load(n, i)[:3]:
                 cp.wait()
-
-            @pl.when(n < 2)
-            def _():
-                load(n, i)[3].wait()
             mix(CORES * j + parity(i), i, jnp.where(i == 0, chips + odd(n), j))
 
             @pl.when(n == 0)
@@ -792,11 +805,11 @@
         slot = lax.rem(unit, slots)
         return remote(send.at[d, slot], recv_ref.at[d, unit], s_sem.at[d, slot], r_sem.at[d, unit], 'tp', jnp.where(d == 0, ring[1], ring[0]))
 
-    def fetch(d, unit):
+    def fetch(d, unit, at):
         ring_copy(d, unit).wait_recv()
-        cp = pltpu.make_async_copy(recv_ref.at[d, unit], rbuf, l_sem)
+        cp = pltpu.make_async_copy(recv_ref.at[d, unit], rbuf.at[at], l_sem.at[at])
         cp.start()
-        cp.wait()
+        return cp
 
     def o_copy(d, b):
         cols = rows_at(d * half_cols + b * wc, wc)
@@ -806,22 +819,25 @@
         return dot32(va_own[dest], wbuf[slot, 0]) + dot32(va_par[dest], wbuf[slot, 1])
 
     def finish(d, b):
-        fetch(d, (hops - 1) * nb + b)
-        cols = rows_at(d * half_cols + b * wc, wc)
-        xo[:, cols] = (xo[:, cols].astype(F32) + (acc[d, lax.rem(b, lag + 1)] + rbuf[...])).astype(BF16)
-        o_copy(d, b).start()
+        last = (hops - 1) * nb + b
+        copies = [fetch(d, last, 0), fetch(flip(d), last - nb, 1)]
+        for cp in copies:
+            cp.wait()
+        cols = rows_at(flip(d) * half_cols + b * wc, wc)
+        xo[:, cols] = (xo[:, cols].astype(F32) + (acc[d, lax.rem(b, lag + 1)] + (rbuf[0] + rbuf[1]))).astype(BF16)
+        o_copy(flip(d), b).start()
 
     def body(u, carry):
         d = odd(u)
-        k = u // (2 * nb)
-        b = lax.rem(u // 2, nb)
+        k = u // (DIRS * nb)
+        b = lax.rem(u // DIRS, nb)
         unit = k * nb + b
         ending = k == hops - 1
 
-        @pl.when((u < 2) | ((b == 0) & (d == 0)))
-        def _():
-            prep(jnp.where(u < 2, u, k + 1))
-        dest = chip_at(jnp.where(d == 0, 2 * chips - 1 - k, 1 + k))
+        @pl.when((d == 0) & ((b == 0) | ((k == 0) & (b == slots + 1))))
+        def _():
+            prep(jnp.where(u == 0, 0, k + 1))
+        dest = chip_at(jnp.where(k == 0, chips // DIRS, jnp.where(d == 0, 1, chips - 1)))
         for cp in w_copies(u):
             cp.wait()
 
@@ -830,7 +846,7 @@
             for cp in w_copies(u + 1):
                 cp.start()
 
-        @pl.when(u == 2)
+        @pl.when(u == DIRS)
         def _():
             x_copy.start()
         part = product(dest, d)
@@ -844,14 +860,14 @@
         def _():
             ring_copy(d, unit - depth).wait_send()
 
-        @pl.when(k == 0)
+        @pl.when(k != 1)
         def _():
             send[d, slot] = part
 
-        @pl.when(k > 0)
-        def _():
-            fetch(d, unit - nb)
-            send[d, slot] = part + rbuf[...]
+        @pl.when(k == 1)
+        def _():
+            fetch(d, unit - nb, 0).wait()
+            send[d, slot] = part + rbuf[0]
         ring_copy(d, unit).start()
 
         @pl.when(ending)
@@ -870,42 +886,42 @@
     lax.fori_loop(0, steps, body, 0)
 
     def tail(i, carry):
-        finish(odd(i), nb - lag + i // 2)
+        finish(odd(i), nb - lag + i // DIRS)
         return carry
 
     def drain(i, carry):
-        o_copy(odd(i), i // 2).wait()
+        o_copy(odd(i), i // DIRS).wait()
         return carry
 
     def drain_send(i, carry):
-        ring_copy(odd(i), hops * nb - depth + i // 2).wait_send()
+        ring_copy(odd(i), hops * nb - depth + i // DIRS).wait_send()
         return carry
-    lax.fori_loop(0, 2 * lag, tail, 0)
-    lax.fori_loop(0, 2 * depth, drain_send, 0)
+    lax.fori_loop(0, DIRS * lag, tail, 0)
+    lax.fori_loop(0, DIRS * depth, drain_send, 0)
     for n in PAIR:
-        swap(2 + n, chip).wait_send()
-    lax.fori_loop(0, 2 * nb, drain, 0)
-
-
-def out_proj_scatter(x_act, bc_act, cum, cl, seg_row, seg_prev, sloc, pd, s_in, z_arr, x_full, w_z, d_skip, norm_w, w_own, w_par, x_loc, chips, wc=512, slots=4, zt=256):
+        swap(DIRS + n, chip).wait_send()
+    lax.fori_loop(0, DIRS * nb, drain, 0)
+
+
+def out_proj_scatter(x_act, bc_act, cum, cl, seg_row, seg_prev, sloc, pd, s_in, z_arr, x_full, w_z, d_skip, norm_w, w_own, w_par, x_loc, chips, wc=512, slots=4, zt=256, zlast=1024):
     t, inner = x_act.shape
     rows, d_model = x_loc.shape
     gw = bc_act.shape[1]
     n_state = s_in.shape[0]
-    nb = d_model // 2 // wc
+    nb = d_model // DIRS // wc
     units = (chips - 1) * nb
     return pl.pallas_call(
-        functools.partial(out_kernel, chips, nb, wc, slots, zt),
+        functools.partial(out_kernel, chips, nb, wc, slots, zt, zlast),
         in_specs=[ANY, ANY, VMEM, VMEM, VMEM, VMEM, ANY, VMEM, VMEM, ANY, ANY, ANY, VMEM, VMEM, ANY, ANY, ANY],
         out_specs=[ANY, ANY],
-        out_shape=[out_of(BF16, rows, d_model), out_of(F32, 2, units, rows, wc)],
-        scratch_shapes=[scratch(BF16, chips + 2, rows, inner), scratch(BF16, chips, rows, inner), scratch(BF16, 2, 2, inner, wc), scratch(F32, 2, slots, rows, wc), scratch(F32, 2, slots, rows, wc),
-                        scratch(F32, rows, wc), scratch(BF16, rows, d_model), scratch(BF16, CORES * rows, d_model), scratch(BF16, 2, d_model, zt),
-                        scratch(BF16, CORES, rows, inner), scratch(BF16, 2, rows, inner), scratch(BF16, 2, rows, gw), scratch(F32, 2, n_state, inner),
+        out_shape=[out_of(BF16, rows, d_model), out_of(F32, DIRS, units, rows, wc)],
+        scratch_shapes=[scratch(BF16, chips + DIRS, rows, inner), scratch(BF16, chips, rows, inner), scratch(BF16, DIRS, DIRS, inner, wc), scratch(F32, DIRS, slots, rows, wc), scratch(F32, DIRS, slots, rows, wc),
+                        scratch(F32, DIRS, rows, wc), scratch(BF16, rows, d_model), scratch(BF16, CORES * rows, d_model), scratch(BF16, DIRS, d_model, zt),
+                        scratch(BF16, CORES, rows, inner), scratch(BF16, DIRS, rows, inner), scratch(BF16, DIRS, rows, gw), scratch(F32, DIRS, n_state, inner),
                         scratch(BF16, n_state, inner), scratch(F32, rows, inner), scratch(F32, rows, inner), scratch(F32, 1, inner),
-                        sems(chips), sems(chips), sems(2, 2), sems(2, slots), sems(2, units), DMA, DMA, sems(2, nb), sems(2, 4), sems(2), DMA],
+                        sems(chips), sems(chips), sems(DIRS, DIRS), sems(DIRS, slots), sems(DIRS, units), sems(DIRS), DMA, sems(DIRS, nb), sems(DIRS, 4), sems(DIRS), DMA],
         compiler_params=params(63, 1),
-        cost_estimate=pl.CostEstimate(flops=2 * t * inner * d_model, bytes_accessed=t * d_model, transcendentals=0),
+        cost_estimate=pl.CostEstimate(flops=DIRS * t * inner * d_model, bytes_accessed=t * d_model, transcendentals=0),
         name='out_proj_scatter',
     )(x_act, bc_act, cum, cl, seg_row, seg_prev, sloc, pd, s_in, z_arr, x_full, w_z, d_skip, norm_w, w_own, w_par, x_loc)[0]
 

time: 544 us -> 529 us (0.972)
  Pallas kernels: 538 us -> 524 us
    pallas_call x1, Pallas kernels: 45.7 us -> 36.3 us  [z_chain(): pl.pallas_call(functools.partial(chain_kernel, chips, blocks, pieces, hop...]
where the time goes in v4:
time: 529 us; the launch traced here: 528 us
  Pallas kernels  524 us (99%)
    pallas_call x1, Pallas kernels, out_proj_scatter(): pl.pallas_call(functools.partial(out_kernel, chips, nb, wc, slots, zt, zl...  294 us
    pallas_call x1, Pallas kernels, gather_proj(): pl.pallas_call(functools.partial(gather_kernel, chips, blocks, kb, nb, su...  164 us
    pallas_call x1, Pallas kernels, z_chain(): pl.pallas_call(functools.partial(chain_kernel, chips, blocks, pieces, hop...  36.3 us
    pallas_call x1, Pallas kernels, phase_a(): pl.pallas_call(functools.partial(phase_a_kernel, q), grid=(nt,), in_specs...  29.5 us

profile of v4, /device:TPU:97, one launch (start us, length us, event | category | flops | bytes accessed | tf_op | source)
XLA Modules:
  0.0 528.4 jit_solution(10280514809187725138)
XLA Ops:
  0.0 164.3 %gather_proj.1 = (bf16[2048,8192]{1,0:T(8,128)(2,1)}, bf16[2048,2048]{1,0:T(8,128)(2,1)}, bf16[2048,384]{1,0:T(8,128)(2,1)}, bf16[8192,2048]{1,0:T(8,128)(2,1)},...) custom-call(bf16[256,8192]{1,0:T(8,128)(2,1)} %x_ref.3, ...), custom_call_target="tpu_custom_call" | custom-call | flops 34359738368 | bytes 4194304 | tf_op jit(solution)/shard_map/gather_proj/pallas_call | solution.py:404
  164.3 29.5 %phase_a.1 = (bf16[2048,2048]{1,0:T(8,128)(2,1)}, bf16[2048,256]{1,0:T(8,128)(2,1)}, f32[32,2048]{1,0:T(8,128)}, f32[32,2048]{1,0:T(8,128)}, f32[1,2048]{1,0:T(1...) custom-call(bf16[2048,2048]{1,0:T(8,128)(2,1)} %get-tuple-element.27, ...), custom_call_target="tpu_custom_call" | custom-call | flops 1073741824 | bytes 4194304 | tf_op jit(solution)/shard_map/phase_a/pallas_call | solution.py:515
  193.8 36.3 %z_chain.1 = (bf16[2048,2048]{1,0:T(8,128)(2,1)}, f32[128,2048]{1,0:T(8,128)}) custom-call(bf16[2048,8192]{1,0:T(8,128)(2,1)} %get-tuple-element.41.xf_ref, bf16[8192,2048]{1,0:T(8,128)(2,1)} %get-tuple-element.42.wz_ref, f32[128,2048]{1,0:T(8,128)} %get-tuple-element.43.send_ref, f32[1,2048]{1,0:T(1,128)} %get-tuple-element.44.dec_ref), custom_call_target="tpu_custom_call" | custom-call | flops 34359738368 | bytes 4194304 | tf_op jit(solution)/shard_map/z_chain/pallas_call | solution.py:636
  230.1 293.6 %out_proj_scatter.1 = (bf16[256,8192]{1,0:T(8,128)(2,1)}, f32[2,24,256,512]{3,2,1,0:T(8,128)}) custom-call(bf16[2048,2048]{1,0:T(8,128)(2,1)} %get-tuple-element.33.xact_ref, bf16[2048,256]{1,0:T(8,128)(2,1)} %get-tuple-element.34.bc_ref, f32[32,2048]{1,0:T(8,128)} %get-tuple-element.35.cum_ref, f32[32,2048]{1,0:T(8,128)} %get-tuple-element.36.cl_ref, ...), custom_call_target="tpu_custom_call" | custom-call | flops 68719476736 | bytes 16777216 | tf_op jit(solution)/shard_map/out_proj_scatter/pallas_call | solution.py:913
  523.8 4.6 copy.16

commit v5 on v4

--- a/solution.py
+++ b/solution.py
@@ -360,16 +360,50 @@
             for cp in halo_copies(slot):
                 cp.start()
 
-        @pl.when((lv >= early) & (lv < last))
+        @pl.when(lv >= early)
         def _():
             take(lv + 1)
+
+        @pl.when((lv >= early) & (lv < last - 1))
+        def _():
             fetch(lv + 1)
+
+        @pl.when(lv == last - 1)
+        def _():
+            for b in PAIR:
+                load(last, b).start()
         return carry
-    lax.fori_loop(0, last + 1, round_body, 0)
+    lax.fori_loop(0, last, round_body, 0)
+
+    slot = last % CORES
+    for cp in out_copies(last - CORES):
+        cp.wait()
+    copies = out_copies(last)
+    for part in PAIR:
+        for b in PAIR:
+            load(last, CORES * part + b).wait()
+        some = pl.ds(part * CORES * qr, CORES * qr)
+
+        def half_dots(n, carry, part=part, some=some):
+            if part == 0:
+                @pl.when(n == 1)
+                def _():
+                    for side in PAIR:
+                        pair_arrival(last, side).wait_recv()
+                        load(last, CORES + side).start()
+            cols = rows_at(n * nt, nt)
+            ost[slot, some, cols] = dot32(xg[slot, some, :], wx[:, cols]).astype(BF16)
+            return carry
+        lax.fori_loop(0, inner // nt, half_dots, 0)
+        bst[slot, some, :] = dot32(xg[slot, some, :], wsm[...]).astype(BF16)
+        for cp in copies[part * quarters:(part + 1) * quarters]:
+            cp.start()
 
     @pl.when(halo_lv == last)
     def _():
-        for cp in halo_copies(last % CORES):
+        for cp in halo_copies(slot):
+            cp.start()
+        for cp in halo_copies(slot):
             cp.wait_send()
     for cp in halo_copies(0):
         cp.wait_recv()

time: 529 us -> 527 us (level)
  no operation moved by 1% of the time
where the time goes in v5:
time: 527 us; the launch traced here: 525 us
  Pallas kernels  521 us (99%)
    pallas_call x1, Pallas kernels, out_proj_scatter(): pl.pallas_call(functools.partial(out_kernel, chips, nb, wc, slots, zt, zl...  293 us
    pallas_call x1, Pallas kernels, gather_proj(): pl.pallas_call(functools.partial(gather_kernel, chips, blocks, kb, nb, su...  162 us
    pallas_call x1, Pallas kernels, z_chain(): pl.pallas_call(functools.partial(chain_kernel, chips, blocks, pieces, hop...  36.3 us
    pallas_call x1, Pallas kernels, phase_a(): pl.pallas_call(functools.partial(phase_a_kernel, q), grid=(nt,), in_specs...  29.5 us

profile of v5, /device:TPU:97, one launch (start us, length us, event | category | flops | bytes accessed | tf_op | source)
XLA Modules:
  0.0 525.4 jit_solution(6689362301843545812)
XLA Ops:
  0.0 161.5 %gather_proj.1 = (bf16[2048,8192]{1,0:T(8,128)(2,1)}, bf16[2048,2048]{1,0:T(8,128)(2,1)}, bf16[2048,384]{1,0:T(8,128)(2,1)}, bf16[8192,2048]{1,0:T(8,128)(2,1)},...) custom-call(bf16[256,8192]{1,0:T(8,128)(2,1)} %x_ref.3, ...), custom_call_target="tpu_custom_call" | custom-call | flops 34359738368 | bytes 4194304 | tf_op jit(solution)/shard_map/gather_proj/pallas_call | solution.py:438
  161.5 29.5 %phase_a.1 = (bf16[2048,2048]{1,0:T(8,128)(2,1)}, bf16[2048,256]{1,0:T(8,128)(2,1)}, f32[32,2048]{1,0:T(8,128)}, f32[32,2048]{1,0:T(8,128)}, f32[1,2048]{1,0:T(1...) custom-call(bf16[2048,2048]{1,0:T(8,128)(2,1)} %get-tuple-element.27, ...), custom_call_target="tpu_custom_call" | custom-call | flops 1073741824 | bytes 4194304 | tf_op jit(solution)/shard_map/phase_a/pallas_call | solution.py:549
  191.1 36.3 %z_chain.1 = (bf16[2048,2048]{1,0:T(8,128)(2,1)}, f32[128,2048]{1,0:T(8,128)}) custom-call(bf16[2048,8192]{1,0:T(8,128)(2,1)} %get-tuple-element.41.xf_ref, bf16[8192,2048]{1,0:T(8,128)(2,1)} %get-tuple-element.42.wz_ref, f32[128,2048]{1,0:T(8,128)} %get-tuple-element.43.send_ref, f32[1,2048]{1,0:T(1,128)} %get-tuple-element.44.dec_ref), custom_call_target="tpu_custom_call" | custom-call | flops 34359738368 | bytes 4194304 | tf_op jit(solution)/shard_map/z_chain/pallas_call | solution.py:670
  227.4 293.4 %out_proj_scatter.1 = (bf16[256,8192]{1,0:T(8,128)(2,1)}, f32[2,24,256,512]{3,2,1,0:T(8,128)}) custom-call(bf16[2048,2048]{1,0:T(8,128)(2,1)} %get-tuple-element.33.xact_ref, bf16[2048,256]{1,0:T(8,128)(2,1)} %get-tuple-element.34.bc_ref, f32[32,2048]{1,0:T(8,128)} %get-tuple-element.35.cum_ref, f32[32,2048]{1,0:T(8,128)} %get-tuple-element.36.cl_ref, ...), custom_call_target="tpu_custom_call" | custom-call | flops 68719476736 | bytes 16777216 | tf_op jit(solution)/shard_map/out_proj_scatter/pallas_call | solution.py:947
  520.8 4.6 copy.16
